TPU v7x, 32 devices: a whole 2x2x4 slice. The times are simulated.
32 devices in a mesh: expert: 4 (over y, x), dp: 8 (over z, core).
Axes of the slice: x: 2, y: 2, z: 4, core: 2. Of those that a mesh axis runs over, the one named last changes fastest.
Arguments:
- pool_tokens: bfloat16 [16384, 2048], P('dp', 'expert'), may hold values from -6 to 6
- pool_cotangent: bfloat16 [16384, 2048], P('dp', 'expert'), may hold values from -6 to 6
- token_ids: int32 [4, 4096], P('expert', 'dp'), may hold values from 0 to 2047, as said below
- route_weights: float32 [4, 4096], P('expert', 'dp'), may hold values from 0.1 to 1
- gate_weight: float32 [4, 2048, 512], P('expert', 'dp'), may hold values from -0.125 to 0.125
- up_weight: float32 [4, 2048, 512], P('expert', 'dp'), may hold values from -0.125 to 0.125
- down_weight: float32 [4, 512, 2048], P('expert', 'dp'), may hold values from -0.25 to 0.25
- momentum_gate: float32 [4, 2048, 512], P('expert', 'dp'), may hold values from -0.6 to 0.6
- momentum_up: float32 [4, 2048, 512], P('expert', 'dp'), may hold values from -0.6 to 0.6
- momentum_down: float32 [4, 512, 2048], P('expert', 'dp'), may hold values from -0.6 to 0.6
Outputs:
- new_gate: float32 [4, 2048, 512], P('expert', 'dp')
- new_up: float32 [4, 2048, 512], P('expert', 'dp')
- new_down: float32 [4, 512, 2048], P('expert', 'dp')
- new_momentum_gate: float32 [4, 2048, 512], P('expert', 'dp')
- new_momentum_up: float32 [4, 2048, 512], P('expert', 'dp')
- new_momentum_down: float32 [4, 512, 2048], P('expert', 'dp')
- pool_grad: float32 [16384, 2048], P('dp', 'expert')
Inputs may be any that keep to these rules, and one draw needn't show every extreme that they name: `token_ids`: within one expert's 512 slots of one dp index the ids are distinct rows of that index's pool.
All inputs are finite; a program needn't handle non-finite values.
Results may differ from a plain program's by a relative error of at most 0.0066.
Values may be sent and summed in bfloat16 or wider, within the bound.
A program may use at most 128 MiB of HBM per device.

v0:
```python
import functools

import jax
import jax.numpy as jnp
from jax import lax
from jax.experimental import pallas as pl
from jax.experimental.pallas import tpu as pltpu
from jax.sharding import PartitionSpec as P


momentum_decay = 0.9
learning_rate = 0.05
epsilon = 1e-06

def dot(left, right, dims, kind=jnp.float32):
    return lax.dot_general(
        left, right, ((dims[0], dims[1]), ((), ())), preferred_element_type=jnp.float32
    ).astype(kind)


def coefs(inner, norm):
    return 1.0 - inner / (2.0 * (norm + epsilon))


def merge_kernel(
    n_e, n_dp, hid,
    full_gu, full_dn, slot_grad, ids,
    pool_out, gu_out, dn_out,
    sent_gu, sent_dn, returned, stats, stats_in, own_gu, own_dn, out_gu, out_dn, in_gu, in_dn,
    ret_send, ret_recv, blk_send, blk_recv, st_send, st_recv,
):
    f32, bf16 = jnp.float32, jnp.bfloat16
    MESH = pl.DeviceIdType.MESH
    me, me_e = lax.axis_index("dp"), lax.axis_index("expert")
    tiers = n_dp.bit_length() - 1
    slots = slot_grad.shape[0]
    width = slot_grad.shape[1] // n_e
    rows_gu, rows_dn = full_gu.shape[1], full_dn.shape[1]
    step_rows = 16

    barrier = pltpu.get_barrier_semaphore()
    for d in range(1, n_dp):
        pl.semaphore_signal(barrier, inc=1, device_id={"dp": me ^ d}, device_id_type=MESH)
    for d in range(1, n_e):
        pl.semaphore_signal(barrier, inc=1, device_id={"expert": me_e ^ d}, device_id_type=MESH)
    pl.semaphore_wait(barrier, n_dp + n_e - 2)

    pending = []

    def send(src, dst, ssem, rsem, device):
        copy = pltpu.make_async_remote_copy(
            src_ref=src, dst_ref=dst, send_sem=ssem, recv_sem=rsem, device_id=device, device_id_type=MESH
        )
        copy.start()
        pending.append(copy)
        return copy

    offset, start = [], 0
    for tier in range(tiers):
        offset.append(start)
        start += 2 * (n_dp >> (tier + 1))

    def send_block(tier, j):
        peer = {"dp": me ^ (1 << tier)}
        src_gu, src_dn = (sent_gu, sent_dn) if tier == 0 else (out_gu[tier - 1], out_dn[tier - 1])
        at = offset[tier] + 2 * j
        return (
            send(src_gu.at[j], in_gu[tier].at[j], blk_send.at[at], blk_recv.at[at], peer),
            send(src_dn.at[j], in_dn[tier].at[j], blk_send.at[at + 1], blk_recv.at[at + 1], peer),
        )

    flying = []
    for j in range(n_dp // 2):
        away = 2 * j + 1 - (me & 1)
        sent_gu[j] = full_gu[away].astype(bf16)
        sent_dn[j] = full_dn[away].astype(bf16)
        flying.append(send_block(0, j))
    back = [None]
    for d in range(1, n_e):
        col = pl.multiple_of((me_e ^ d) * width, width)
        back.append(
            send(
                slot_grad.at[:, pl.ds(col, width)],
                returned.at[pl.ds(d * slots, slots)],
                ret_send.at[d], ret_recv.at[d], {"expert": me_e ^ d},
            )
        )
    returned[pl.ds(0, slots), :] = slot_grad[:, pl.ds(pl.multiple_of(me_e * width, width), width)]

    def pool_sum():
        for copy in back[1:]:
            copy.wait_recv()
        tile = 256

        @pl.loop(0, pool_out.shape[0] // tile)
        def _(t):
            at = pl.multiple_of(t * tile, tile)
            row = lax.broadcasted_iota(jnp.int32, (tile, n_e * slots), 0) + at
            pick = jnp.where(row == ids[...], 1.0, 0.0).astype(bf16)
            pool_out[pl.ds(at, tile), :] = jnp.dot(pick, returned[...], preferred_element_type=f32)

    def accumulate(mine, at_mine, other, rows, j, acc):
        def body(t, acc):
            at = pl.ds(pl.multiple_of(t * step_rows, step_rows), step_rows)
            a = mine[at_mine, at, :]
            b = other[j, at, :].astype(f32)

            def fold(x):
                return x[:8] + x[8:]

            return acc[0] + fold(a * b), acc[1] + fold(a * a), acc[2] + fold(b * b)

        return lax.fori_loop(0, rows // step_rows, body, acc)

    def lanes(x):
        total = x[:, :128]
        for c in range(1, x.shape[1] // 128):
            total = total + x[:, c * 128 : (c + 1) * 128]
        return jnp.sum(total, axis=0, keepdims=True)

    mine_gu, mine_dn = full_gu, full_dn
    for tier in range(tiers):
        blocks = n_dp >> (tier + 1)
        bit = (me >> tier) & 1

        def place(j, tier=tier, bit=bit):
            return 2 * j + bit if tier == 0 else j

        if tier == tiers - 1:
            pool_sum()
        acc_gu = tuple(jnp.zeros((8, 2 * hid), f32) for _ in range(3))
        acc_dn = tuple(jnp.zeros((8, full_dn.shape[2]), f32) for _ in range(3))
        for j in range(blocks):
            flying[j][0].wait_recv()
            acc_gu = accumulate(mine_gu, place(j), in_gu[tier], rows_gu, j, acc_gu)
        for j in range(blocks):
            flying[j][1].wait_recv()
            acc_dn = accumulate(mine_dn, place(j), in_dn[tier], rows_dn, j, acc_dn)
        parts = [[lanes(acc_gu[i][:, :hid]), lanes(acc_gu[i][:, hid:]), lanes(acc_dn[i])] for i in range(3)]
        left = [jnp.where(bit == 0, m, o) for m, o in zip(parts[1], parts[2])]
        right = [jnp.where(bit == 0, o, m) for m, o in zip(parts[1], parts[2])]
        local_stats = jnp.concatenate(
            [*parts[0], *left, *right, jnp.zeros((7, 128), f32)], axis=0
        )
        stats[tier] = local_stats
        group = 2 << tier
        first = group - 2 - tier
        news = [
            send(
                stats.at[tier], stats_in.at[first + d - 1],
                st_send.at[first + d - 1], st_recv.at[first + d - 1], {"dp": me ^ d},
            )
            for d in range(1, group)
        ]
        total = local_stats
        for d in range(1, group):
            news[d - 1].wait_recv()
            total = total + stats_in[first + d - 1]
        whole = jnp.sum(total, axis=1, keepdims=True)
        inner = whole[0:3]
        c_left, c_right = coefs(inner, whole[3:6]), coefs(inner, whole[6:9])
        c_mine = jnp.where(bit == 0, c_left, c_right)
        c_other = jnp.where(bit == 0, c_right, c_left)

        def spread(c):
            return jnp.concatenate(
                [jnp.broadcast_to(c[0:1], (1, hid)), jnp.broadcast_to(c[1:2], (1, hid))], axis=1
            ), c[2:3]

        (gu_m, dn_m), (gu_o, dn_o) = spread(c_mine), spread(c_other)

        def combine(mine, other, rows, j, c_m, c_o, store):
            def body(t, carry):
                at = pl.ds(pl.multiple_of(t * step_rows, step_rows), step_rows)
                store(at, mine[place(j), at, :] * c_m + other[j, at, :].astype(f32) * c_o)
                return carry

            lax.fori_loop(0, rows // step_rows, body, 0)

        def storer(ref, j):
            def store(at, value):
                ref[j, at, :] = value.astype(ref.dtype)

            return store

        def store_gu(at, value):
            gu_out[at, :] = value

        def store_dn(at, value):
            dn_out[at, :] = value

        if tier == tiers - 1:
            combine(mine_gu, in_gu[tier], rows_gu, 0, gu_m, gu_o, store_gu)
            combine(mine_dn, in_dn[tier], rows_dn, 0, dn_m, dn_o, store_dn)
        else:
            up = (me >> (tier + 1)) & 1
            flying = []
            for j in range(blocks // 2):
                combine(mine_gu, in_gu[tier], rows_gu, 2 * j + 1 - up, gu_m, gu_o, storer(out_gu[tier], j))
                combine(mine_dn, in_dn[tier], rows_dn, 2 * j + 1 - up, dn_m, dn_o, storer(out_dn[tier], j))
                flying.append(send_block(tier + 1, j))
            for j in range(blocks // 2):
                combine(mine_gu, in_gu[tier], rows_gu, 2 * j + up, gu_m, gu_o, storer(own_gu[tier], j))
                combine(mine_dn, in_dn[tier], rows_dn, 2 * j + up, dn_m, dn_o, storer(own_dn[tier], j))
            mine_gu, mine_dn = own_gu[tier], own_dn[tier]
    for copy in pending:
        copy.wait_send()


def merged(grads, slot_grad, ids_back, pool_rows, n_e, n_dp, hid):
    f32, bf16 = jnp.float32, jnp.bfloat16
    gu, dn = grads[0].shape[1:], grads[1].shape[1:]
    slots, full = slot_grad.shape
    tiers = n_dp.bit_length() - 1
    n_blocks = sum(2 * (n_dp >> (t + 1)) for t in range(tiers))
    n_stats = sum((2 << t) - 1 for t in range(tiers))
    vmem = pl.BlockSpec(memory_space=pltpu.VMEM)

    def per_tier(shape, kind, first):
        return [pltpu.VMEM((n_dp >> (t + 1), *shape), kind) for t in range(first, tiers)]

    return pl.pallas_call(
        functools.partial(merge_kernel, n_e, n_dp, hid),
        out_shape=(
            jax.ShapeDtypeStruct((pool_rows, full // n_e), f32),
            jax.ShapeDtypeStruct(gu, f32),
            jax.ShapeDtypeStruct(dn, f32),
        ),
        in_specs=[vmem] * 4,
        out_specs=(vmem,) * 3,
        scratch_shapes=[
            pltpu.VMEM((n_dp // 2, *gu), bf16),
            pltpu.VMEM((n_dp // 2, *dn), bf16),
            pltpu.VMEM((n_e * slots, full // n_e), bf16),
            pltpu.VMEM((tiers, 16, 128), f32),
            pltpu.VMEM((n_stats, 16, 128), f32),
            per_tier(gu, f32, 1),
            per_tier(dn, f32, 1),
            per_tier(gu, bf16, 1),
            per_tier(dn, bf16, 1),
            per_tier(gu, bf16, 0),
            per_tier(dn, bf16, 0),
            pltpu.SemaphoreType.DMA((n_e,)),
            pltpu.SemaphoreType.DMA((n_e,)),
            pltpu.SemaphoreType.DMA((n_blocks,)),
            pltpu.SemaphoreType.DMA((n_blocks,)),
            pltpu.SemaphoreType.DMA((n_stats,)),
            pltpu.SemaphoreType.DMA((n_stats,)),
        ],
        compiler_params=pltpu.CompilerParams(
            collective_id=1, has_side_effects=True, vmem_limit_bytes=60 * 1024 * 1024
        ),
    )(grads[0], grads[1], slot_grad, ids_back)


def gather_kernel(
    n_e, n_dp,
    ids, tokens, cot, shard_gu, shard_dn,
    routed, cot_rows, gu_full, dn_full, all_ids,
    stage_x, stage_c,
    id_send, id_recv, tok_send, tok_recv, line_send, line_recv, pair_send, pair_recv,
):
    f32, bf16 = jnp.float32, jnp.bfloat16
    MESH = pl.DeviceIdType.MESH
    me, me_e = lax.axis_index("dp"), lax.axis_index("expert")
    chips = n_dp // 2
    chip, core = me // 2, me % 2
    slots = ids.shape[1]
    pool_rows, width = tokens.shape

    barrier = pltpu.get_barrier_semaphore()
    for d in range(1, n_e):
        pl.semaphore_signal(barrier, inc=1, device_id={"expert": me_e ^ d}, device_id_type=MESH)
    pl.semaphore_signal(barrier, inc=1, device_id={"dp": me ^ 1}, device_id_type=MESH)
    for way in (-1, 1):
        pl.semaphore_signal(
            barrier, inc=1, device_id={"dp": lax.rem(me + 2 * way + n_dp, n_dp)}, device_id_type=MESH
        )
    pl.semaphore_wait(barrier, n_e + 2)

    def remote(src, dst, ssem, rsem, device):
        return pltpu.make_async_remote_copy(
            src_ref=src, dst_ref=dst, send_sem=ssem, recv_sem=rsem, device_id=device, device_id_type=MESH
        )

    pending = []
    id_copies = [None]
    for d in range(1, n_e):
        copy = remote(ids, all_ids.at[d], id_send.at[d], id_recv.at[d], {"expert": me_e ^ d})
        copy.start()
        id_copies.append(copy)
        pending.append(copy)
    all_ids[0] = ids[...]

    fulls = (gu_full, dn_full)
    shards = (shard_gu, shard_dn)

    def along(way, hop, part):
        side = 0 if way > 0 else 1
        origin = me - 2 * way * hop
        src = shards[part] if hop == 0 else fulls[part].at[origin]
        return remote(
            src, fulls[part].at[origin],
            line_send.at[side, hop, part], line_recv.at[side, hop, part], {"dp": me + 2 * way},
        )

    def arriving(way, hop, part):
        side = 0 if way > 0 else 1
        origin = me - 2 * way * (hop + 1)
        return remote(
            fulls[part].at[origin], fulls[part].at[origin],
            line_send.at[side, hop, part], line_recv.at[side, hop, part], {"dp": me ^ 1},
        )

    def across(way, hop, part):
        side = 0 if way > 0 else 1
        origin = me - 2 * way * hop
        src = shards[part] if hop == 0 else fulls[part].at[origin]
        return remote(
            src, fulls[part].at[origin],
            pair_send.at[side, hop, part], pair_recv.at[side, hop, part], {"dp": me ^ 1},
        )

    def across_arriving(way, hop, part):
        side = 0 if way > 0 else 1
        origin = (me ^ 1) - 2 * way * hop
        return remote(
            fulls[part].at[origin], fulls[part].at[origin],
            pair_send.at[side, hop, part], pair_recv.at[side, hop, part], {"dp": me ^ 1},
        )

    def has(way, hop):
        behind = chip >= hop if way > 0 else chip < chips - hop
        ahead = chip < chips - 1 if way > 0 else chip >= 1
        return behind, ahead

    for part in (0, 1):
        for way in (1, -1):
            @pl.when(has(way, 0)[1])
            def _(way=way, part=part):
                along(way, 0, part).start()
    for part in (0, 1):
        across(1, 0, part).start()

    tok_copies = []

    def pick(d):
        column = jnp.transpose(jnp.broadcast_to(all_ids[d], (128, slots)))
        lane = lax.broadcasted_iota(jnp.int32, (slots, 128), 1)
        cols = [
            jnp.where(column == lane + c * 128, 1.0, 0.0).astype(bf16) for c in range(pool_rows // 128)
        ]
        chosen = jnp.concatenate(cols, axis=1)
        stage_x[d] = jnp.dot(chosen, tokens[...], preferred_element_type=f32).astype(bf16)
        stage_c[d] = jnp.dot(chosen, cot[...], preferred_element_type=f32).astype(bf16)

    own = pl.ds(pl.multiple_of(me_e * width, width), width)
    for d in range(1, n_e):
        id_copies[d].wait_recv()
        pick(d)
        for part, (stage, land) in enumerate(((stage_x, routed), (stage_c, cot_rows))):
            copy = remote(
                stage.at[d], land.at[:, own], tok_send.at[d, part], tok_recv.at[d, part], {"expert": me_e ^ d}
            )
            copy.start()
            tok_copies.append((d, part))
            pending.append(copy)
    pick(0)
    routed[:, own] = stage_x[0]
    cot_rows[:, own] = stage_c[0]
    gu_full[me] = shard_gu[...]
    dn_full[me] = shard_dn[...]

    for hop in range(chips - 1):
        for part in (0, 1):
            for way in (1, -1):
                behind, ahead = has(way, hop + 1)

                @pl.when(behind)
                def _(way=way, hop=hop, part=part):
                    arriving(way, hop, part).wait_recv()
                    across(way, hop + 1, part).start()

                @pl.when(jnp.logical_and(behind, ahead))
                def _(way=way, hop=hop, part=part):
                    along(way, hop + 1, part).start()

    for d, part in tok_copies:
        land = (routed, cot_rows)[part]
        theirs = pl.ds(pl.multiple_of((me_e ^ d) * width, width), width)
        stage = (stage_x, stage_c)[part]
        remote(
            stage.at[d], land.at[:, theirs], tok_send.at[d, part], tok_recv.at[d, part], {"expert": me_e ^ d}
        ).wait_recv()
    for part in (0, 1):
        across_arriving(1, 0, part).wait_recv()
        across(1, 0, part).wait_send()
    for hop in range(chips):
        for part in (0, 1):
            for way in (1, -1):
                behind, ahead = has(way, hop)

                @pl.when(jnp.logical_and(behind, ahead))
                def _(way=way, hop=hop, part=part):
                    along(way, hop, part).wait_send()

                if hop:
                    @pl.when(behind)
                    def _(way=way, hop=hop, part=part):
                        across_arriving(way, hop, part).wait_recv()
                        across(way, hop, part).wait_send()
    for copy in pending:
        copy.wait_send()


def gathered(ids, tokens, cot, shard_gu, shard_dn, n_e, n_dp):
    bf16 = jnp.bfloat16
    slots, width = ids.shape[1], tokens.shape[1]
    chips = n_dp // 2
    vmem = pl.BlockSpec(memory_space=pltpu.VMEM)
    dma = pltpu.SemaphoreType.DMA
    return pl.pallas_call(
        functools.partial(gather_kernel, n_e, n_dp),
        out_shape=(
            jax.ShapeDtypeStruct((slots, n_e * width), bf16),
            jax.ShapeDtypeStruct((slots, n_e * width), bf16),
            jax.ShapeDtypeStruct((n_dp, *shard_gu.shape), bf16),
            jax.ShapeDtypeStruct((n_dp, *shard_dn.shape), bf16),
            jax.ShapeDtypeStruct((n_e, *ids.shape), jnp.int32),
        ),
        in_specs=[vmem] * 5,
        out_specs=(vmem,) * 5,
        scratch_shapes=[
            pltpu.VMEM((n_e, slots, width), bf16),
            pltpu.VMEM((n_e, slots, width), bf16),
            dma((n_e,)), dma((n_e,)), dma((n_e, 2)), dma((n_e, 2)),
            dma((2, chips, 2)), dma((2, chips, 2)), dma((2, chips, 2)), dma((2, chips, 2)),
        ],
        compiler_params=pltpu.CompilerParams(
            collective_id=2, has_side_effects=True, vmem_limit_bytes=60 * 1024 * 1024
        ),
    )(ids, tokens, cot, shard_gu, shard_dn)


def local(
    pool_tokens,
    pool_cotangent,
    token_ids,
    route_weights,
    gate_weight,
    up_weight,
    down_weight,
    momentum_gate,
    momentum_up,
    momentum_down,
):
    bf16, f32 = jnp.bfloat16, jnp.float32
    n_e = lax.axis_size("expert")
    n_dp = lax.axis_size("dp")
    pool_rows = pool_tokens.shape[0]
    slots = token_ids.shape[1]
    hid = gate_weight.shape[2]
    shard_gu = jnp.concatenate([gate_weight[0], up_weight[0]], axis=1).astype(bf16)
    routed, cot_rows, gu_full, down_full, ids_back = gathered(
        token_ids, pool_tokens, pool_cotangent, shard_gu, down_weight[0].astype(bf16), n_e, n_dp
    )
    gu_full = gu_full.reshape(-1, 2 * hid)
    down_full = down_full.reshape(hid, -1)

    route = route_weights[0]
    scaled_cot = (route[:, None] * cot_rows.astype(f32)).astype(bf16)
    pre = dot(routed, gu_full, ((1,), (0,)))
    gate_pre, up_pre = pre[:, :hid], pre[:, hid:]
    sig = jax.nn.sigmoid(gate_pre)
    act = gate_pre * sig
    hidden = (act * up_pre).astype(bf16)
    hidden_grad = dot(scaled_cot, down_full, ((1,), (1,)))
    gate_grad = (hidden_grad * up_pre * sig * (1.0 + gate_pre * (1.0 - sig))).astype(bf16)
    up_grad = (hidden_grad * act).astype(bf16)
    both_grad = jnp.concatenate([gate_grad, up_grad], axis=1)

    grads = (
        (dot(routed, both_grad, ((0,), (0,))) / slots).reshape(n_dp, -1, 2 * hid),
        (dot(hidden, scaled_cot, ((0,), (0,))) / slots).reshape(n_dp, -1, scaled_cot.shape[1]),
    )
    slot_grad = dot(both_grad, gu_full, ((1,), (1,)), bf16)
    pool_grad, fin_gu, fin_dn = merged(grads, slot_grad, ids_back.reshape(1, -1), pool_rows, n_e, n_dp, hid)

    next_gate = momentum_decay * momentum_gate[0] + fin_gu[:, :hid]
    next_up = momentum_decay * momentum_up[0] + fin_gu[:, hid:]
    next_down = momentum_decay * momentum_down[0] + fin_dn
    new_gate = gate_weight[0] - learning_rate * next_gate
    new_up = up_weight[0] - learning_rate * next_up
    new_down = down_weight[0] - learning_rate * next_down
    return (
        new_gate[None],
        new_up[None],
        new_down[None],
        next_gate[None],
        next_up[None],
        next_down[None],
        pool_grad,
    )


def solution(mesh):
    in_specs = (
        P("dp", "expert"),
        P("dp", "expert"),
        P("expert", "dp"),
        P("expert", "dp"),
        P("expert", "dp", None),
        P("expert", "dp", None),
        P("expert", "dp", None),
        P("expert", "dp", None),
        P("expert", "dp", None),
        P("expert", "dp", None),
    )
    out_specs = (
        P("expert", "dp", None),
        P("expert", "dp", None),
        P("expert", "dp", None),
        P("expert", "dp", None),
        P("expert", "dp", None),
        P("expert", "dp", None),
        P("dp", "expert"),
    )
    return jax.shard_map(local, mesh=mesh, in_specs=in_specs, out_specs=out_specs, check_vma=False)
```

profile of v0, /device:TPU:0, one launch (start us, length us, event | category | flops | bytes accessed | tf_op | source)
XLA Modules:
  0.0 196.7 jit_solution(17742774059785667640)
XLA Ops:
  0.6 1.8 bitcast_convert_fusion.shard_dn
  2.4 1.3 bitcast_convert_fusion.1
  3.7 0.9 pad_maximum_fusion.3.shard_gu
  4.6 66.3 %shard_map.153 = (bf16[512,2048]{1,0:T(8,128)(2,1)}, bf16[512,2048]{1,0:T(8,128)(2,1)}, bf16[8,256,1024]{2,1,0:T(8,128)(2,1)}, bf16[8,64,2048]{2,1,0:T(8,128)(2,1)}, s32[4,1,512]{2,1,0:T(1,128)}) custom-call(s32[1,512]{1,0:T(1,128)} %ids.1, bf16[2048,512]{1,0:T(8,128)(2,1)} %tokens.1, bf16[2048,512]{1,0:T(8,128)(2,1)} %cot.1, ...), custom_call_target="tpu_custom_call" | custom-call | tf_op jit(solution)/shard_map/pallas_call | solution.py:422
  70.9 0.0 copy-start.9
  70.9 0.0 copy-start.10
  71.0 0.0 copy-start.11
  71.0 5.3 %fusion.12 = f32[512,1024]{0,1:T(8,128)S(1)} fusion(bf16[512,2048]{1,0:T(8,128)(2,1)} %get-tuple-element.15, bf16[2048,1024]{1,0:T(8,128)(2,1)} %bitcast.59), kind=kOutput, calls=%fused_computation.30 | convolution fusion | flops 2147483648 | bytes 8388608 | tf_op jit(solution)/shard_map/dot_general | solution.py:16
  76.3 0.0 copy-done.9
  76.3 0.0 copy-done.10
  76.3 0.0 copy-done.11
  76.4 0.0 copy-start.7
  76.4 1.7 multiply_convert_fusion.3
  78.0 0.5 copy-done.7
  78.5 4.0 %convolution_convert_fusion.slot_grad = bf16[512,2048]{1,0:T(8,128)(2,1)} fusion(bf16[2048,1024]{1,0:T(8,128)(2,1)S(1)} %bitcast.60, bf16[512,512]{0,1:T(8,128)(2,1)S(1)} %get-tuple-element.24, bf16[512,512]{0,1:T(8,128)(2,1)S(1)} %get-tuple-element.23), kind=kOutput, calls=%fused_computation.3 | convolution fusion | flops 2150629376 | bytes 7340032 | tf_op jit(solution)/shard_map/dot_general | solution.py:16
  82.5 0.0 copy-start.8
  82.5 3.5 %convolution_multiply_fusion.1 = f32[512,2048]{1,0:T(8,128)} fusion(bf16[512,2048]{1,0:T(8,128)(2,1)S(1)} %copy-done.9, f32[512]{0:T(512)S(1)} %bitcast.63, f32[512,1024]{0,1:T(8,128)S(1)} %fusion.12), kind=kOutput, calls=%fused_computation.2 | convolution fusion | flops 1079508992 | bytes 8390656 | tf_op jit(solution)/shard_map/dot_general | solution.py:16
  86.0 0.0 copy-done.8
  86.0 5.6 %convolution_multiply_fusion = f32[2048,1024]{1,0:T(8,128)} fusion(bf16[512,2048]{1,0:T(8,128)(2,1)S(1)} %copy-done.8, bf16[512,512]{0,1:T(8,128)(2,1)S(1)} %get-tuple-element.24, bf16[512,512]{0,1:T(8,128)(2,1)S(1)} %get-tuple-element.23), kind=kOutput, calls=%fused_computation | convolution fusion | flops 2151677952 | bytes 11534336 | tf_op jit(solution)/shard_map/dot_general | solution.py:16
  91.7 0.0 copy-start.1
  91.7 0.0 copy-start.2
  91.7 0.0 copy-start.4
  91.7 0.0 copy-start.5
  91.7 97.9 %shard_map.154 = (f32[2048,512]{1,0:T(8,128)}, f32[256,1024]{1,0:T(8,128)}, f32[64,2048]{1,0:T(8,128)}) custom-call(f32[8,256,1024]{2,1,0:T(8,128)} %bitcast.56, f32[8,64,2048]{2,1,0:T(8,128)} %bitcast.57, bf16[512,2048]{1,0:T(8,128)(2,1)} %convolution_convert_fusion.slot_grad, s32[1,2048]{1,0:T(1,128)} %bitcast.58), custom_call_target="tpu_custom_call" | custom-call | tf_op jit(solution)/shard_map/pallas_call | solution.py:222
  189.6 0.0 copy-done.1
  189.6 0.0 copy-done.2
  189.6 0.0 copy-done.4
  189.6 0.0 copy-done.5
  189.7 0.0 copy-start.3
  189.7 0.0 copy-start.6
  189.7 0.0 copy-start
  189.7 2.8 %fusion.7 = (f32[1,256,512]{2,1,0:T(8,128)}, f32[1,256,512]{2,1,0:T(8,128)}, f32[1,256,512]{2,1,0:T(8,128)}, f32[1,256,512]{2,1,0:T(8,128)}) fusion(f32[256,1024]{1,0:T(8,128)} %get-tuple-element.20, f32[1,256,512]{2,1,0:T(8,128)S(1)} %copy-done.4, f32[1,256,512]{2,1,0:T(8,128)S(1)} %copy-done.1, f32[1,256,512]{2,1,0:T(8,128)S(1)} %copy-done.5, ...), kind=kLoop, calls=%fused_computation.26 | loop fusion | flops 1048576 | bytes 5242880 | tf_op jit(solution)/shard_map/broadcast_in_dim | solution.py:500
  192.5 0.0 copy-done.3
  192.5 0.0 copy-done.6
  192.5 2.1 %fusion.5 = (f32[1,64,2048]{2,1,0:T(8,128)}, f32[1,64,2048]{2,1,0:T(8,128)}) fusion(f32[64,2048]{1,0:T(8,128)} %get-tuple-element.21, f32[1,64,2048]{2,1,0:T(8,128)S(1)} %copy-done.6, f32[1,64,2048]{2,1,0:T(8,128)S(1)} %copy-done.3), kind=kLoop, calls=%fused_computation.24 | loop fusion | flops 524288 | bytes 2621440 | tf_op jit(solution)/shard_map/broadcast_in_dim | solution.py:501
  194.7 0.0 copy-done
  194.7 2.0 %copy.21 = f32[2048,512]{1,0:T(8,128)} copy(f32[2048,512]{1,0:T(8,128)S(1)} %copy-done) | data formatting | bytes 8388608
Async XLA Ops:
  70.9 5.4 %copy-start.9 = (bf16[512,2048]{1,0:T(8,128)(2,1)S(1)}, bf16[512,2048]{1,0:T(8,128)(2,1)}, u32[]{:S(2)}) copy-start(bf16[512,2048]{1,0:T(8,128)(2,1)} %get-tuple-element.16) | copy-start | bytes 6291460
  70.9 5.4 %copy-start.10 = (bf16[8,64,2048]{2,1,0:T(8,128)(2,1)S(1)}, bf16[8,64,2048]{2,1,0:T(8,128)(2,1)}, u32[]{:S(2)}) copy-start(bf16[8,64,2048]{2,1,0:T(8,128)(2,1)} %get-tuple-element.17) | copy-start | bytes 6291460
  71.0 5.4 %copy-start.11 = (f32[1,512]{1,0:T(1,128)S(1)}, f32[1,512]{1,0:T(1,128)}, u32[]{:S(2)}) copy-start(f32[1,512]{1,0:T(1,128)} %param.13) | copy-start | bytes 6148
  76.4 2.2 %copy-start.7 = (bf16[8,256,1024]{2,1,0:T(8,128)(2,1)S(1)}, bf16[8,256,1024]{2,1,0:T(8,128)(2,1)}, u32[]{:S(2)}) copy-start(bf16[8,256,1024]{2,1,0:T(8,128)(2,1)} %get-tuple-element.18) | copy-start | bytes 12582916
  82.5 3.5 %copy-start.8 = (bf16[512,2048]{1,0:T(8,128)(2,1)S(1)}, bf16[512,2048]{1,0:T(8,128)(2,1)}, u32[]{:S(2)}) copy-start(bf16[512,2048]{1,0:T(8,128)(2,1)} %get-tuple-element.15) | copy-start | bytes 6291460
  91.7 98.0 %copy-start.1 = (f32[1,256,512]{2,1,0:T(8,128)S(1)}, f32[1,256,512]{2,1,0:T(8,128)}, u32[]{:S(2)}) copy-start(f32[1,256,512]{2,1,0:T(8,128)} %param.15) | copy-start | bytes 1572868
  91.7 98.0 %copy-start.2 = (f32[1,256,512]{2,1,0:T(8,128)S(1)}, f32[1,256,512]{2,1,0:T(8,128)}, u32[]{:S(2)}) copy-start(f32[1,256,512]{2,1,0:T(8,128)} %param.14) | copy-start | bytes 1572868
  91.7 98.0 %copy-start.4 = (f32[1,256,512]{2,1,0:T(8,128)S(1)}, f32[1,256,512]{2,1,0:T(8,128)}, u32[]{:S(2)}) copy-start(f32[1,256,512]{2,1,0:T(8,128)} %param.18) | copy-start | bytes 1572868
  91.7 98.0 %copy-start.5 = (f32[1,256,512]{2,1,0:T(8,128)S(1)}, f32[1,256,512]{2,1,0:T(8,128)}, u32[]{:S(2)}) copy-start(f32[1,256,512]{2,1,0:T(8,128)} %param.17) | copy-start | bytes 1572868
  189.7 2.9 %copy-start.3 = (f32[1,64,2048]{2,1,0:T(8,128)S(1)}, f32[1,64,2048]{2,1,0:T(8,128)}, u32[]{:S(2)}) copy-start(f32[1,64,2048]{2,1,0:T(8,128)} %param.16) | copy-start | bytes 1572868
  189.7 2.9 %copy-start.6 = (f32[1,64,2048]{2,1,0:T(8,128)S(1)}, f32[1,64,2048]{2,1,0:T(8,128)}, u32[]{:S(2)}) copy-start(f32[1,64,2048]{2,1,0:T(8,128)} %param.19) | copy-start | bytes 1572868
  189.7 5.0 %copy-start = (f32[2048,512]{1,0:T(8,128)S(1)}, f32[2048,512]{1,0:T(8,128)}, u32[]{:S(2)}) copy-start(f32[2048,512]{1,0:T(8,128)} %get-tuple-element.48) | copy-start | bytes 12582916
where the time goes:
time: 197 us
  Pallas kernels  164 us (83%)
  matrix products  20.1 us (10%)
  other arithmetic  8.92 us (5%)
  local copies, waits for them, and re-layouts  2.57 us (1%)
    pallas_call x1, Pallas kernels, merged(): pl.pallas_call(functools.partial(merge_kernel, n_e, n_dp, hid), out_shape...  97.9 us
    pallas_call x1, Pallas kernels, gathered(): pl.pallas_call(functools.partial(gather_kernel, n_e, n_dp), out_shape=(ja...  66.3 us
    dot_general x5, matrix products, dot(): lax.dot_general(left, right, ((dims[0], dims[1]), ((), ())), preferred_el...  20.1 us

commit v1 on v0

v1 whole, which is shorter than its diff:
```python
import functools

import jax
import jax.numpy as jnp
from jax import lax
from jax.experimental import pallas as pl
from jax.experimental.pallas import tpu as pltpu
from jax.sharding import PartitionSpec as P


momentum_decay = 0.9
learning_rate = 0.05
epsilon = 1e-06
GATE, UP, DOWN = 0, 1, 2


def coefs(inner, norm):
    return 1.0 - inner / (2.0 * (norm + epsilon))


def chunks_of(blocks):
    return min(2, blocks)


def step_kernel(
    n_e, n_dp,
    ids, route, tok_h, cot_h, gate_h, up_h, down_h, mom_gate_h, mom_up_h, mom_down_h,
    new_gate_h, new_up_h, new_down_h, next_gate_h, next_up_h, next_down_h, pool_h,
    tokens, cot, weights, moments, all_ids, stage_x, stage_c, routed, cot_rows,
    gu_full, dn_full, x_t, h_t, hidden, pre, both, slot_grad, returned, pool,
    own, sent, outs, ins, stats, stats_in,
    in_sem, out_sem, id_send, id_recv, tok_send, tok_recv, line_send, line_recv, pair_send, pair_recv,
    ret_send, ret_recv, blk_send, blk_recv, st_send, st_recv,
):
    f32, bf16 = jnp.float32, jnp.bfloat16
    MESH = pl.DeviceIdType.MESH
    me, me_e = lax.axis_index("dp"), lax.axis_index("expert")
    chips = n_dp // 2
    chip, core = me // 2, me % 2
    tiers = n_dp.bit_length() - 1
    half = n_dp // 2
    slots = ids.shape[1]
    pool_rows, width = tokens.shape
    hid = pre.shape[1] // 2
    rows_gu, rows_dn = gate_h.shape[1], down_h.shape[1]
    rows = (rows_gu, rows_gu, rows_dn)
    cols = (hid, hid, down_h.shape[2])
    lump = min(512, hid)
    peers_e = sorted(range(1, n_e), key=lambda d: -bin(d).count("1"))

    barrier = pltpu.get_barrier_semaphore()
    for d in range(1, n_e):
        pl.semaphore_signal(barrier, inc=1, device_id={"expert": me_e ^ d}, device_id_type=MESH)
    for d in range(1, n_dp):
        pl.semaphore_signal(barrier, inc=1, device_id={"dp": me ^ d}, device_id_type=MESH)

    loads = [
        pltpu.make_async_copy(src, dst, in_sem.at[i])
        for i, (src, dst) in enumerate(
            (
                (gate_h.at[0], weights[GATE]), (up_h.at[0], weights[UP]), (down_h.at[0], weights[DOWN]),
                (tok_h, tokens), (cot_h, cot),
                (mom_gate_h.at[0], moments[GATE]), (mom_up_h.at[0], moments[UP]), (mom_down_h.at[0], moments[DOWN]),
            )
        )
    ]
    for copy in loads:
        copy.start()

    def remote(src, dst, ssem, rsem, device):
        return pltpu.make_async_remote_copy(
            src_ref=src, dst_ref=dst, send_sem=ssem, recv_sem=rsem, device_id=device, device_id_type=MESH
        )

    def block(index, size):
        return pl.ds(pl.multiple_of(index * size, size), size)

    def dot(a, b):
        return jnp.dot(a, b, preferred_element_type=f32)

    def dot_t(a, b):
        return lax.dot_general(a, b, (((1,), (1,)), ((), ())), preferred_element_type=f32)

    pending = []

    def send(*args):
        copy = remote(*args)
        copy.start()
        pending.append(copy)
        return copy

    mine_gu, mine_dn = block(me, rows_gu), block(me, rows_dn)
    loads[0].wait()
    gu_full[mine_gu, :hid] = weights[GATE][...].astype(bf16)
    loads[1].wait()
    gu_full[mine_gu, hid:] = weights[UP][...].astype(bf16)
    loads[2].wait()
    dn_full[mine_dn, :] = weights[DOWN][...].astype(bf16)

    pl.semaphore_wait(barrier, n_e + n_dp - 2)

    id_copies = [None] + [
        send(ids, all_ids.at[d], id_send.at[d], id_recv.at[d], {"expert": me_e ^ d}) for d in range(1, n_e)
    ]
    all_ids[0] = ids[...]

    fulls, shard_rows = (gu_full, dn_full), (rows_gu, rows_dn)

    def shard(part, origin):
        return fulls[part].at[block(origin, shard_rows[part])]

    def along(way, hop, part):
        side = 0 if way > 0 else 1
        origin = me - 2 * way * hop
        return remote(
            shard(part, origin), shard(part, origin),
            line_send.at[side, hop, part], line_recv.at[side, hop, part], {"dp": me + 2 * way},
        )

    def arriving(way, hop, part):
        side = 0 if way > 0 else 1
        origin = me - 2 * way * (hop + 1)
        return remote(
            shard(part, origin), shard(part, origin),
            line_send.at[side, hop, part], line_recv.at[side, hop, part], {"dp": me ^ 1},
        )

    def across(way, hop, part):
        side = 0 if way > 0 else 1
        origin = me - 2 * way * hop
        return remote(
            shard(part, origin), shard(part, origin),
            pair_send.at[side, hop, part], pair_recv.at[side, hop, part], {"dp": me ^ 1},
        )

    def across_arriving(way, hop, part):
        side = 0 if way > 0 else 1
        origin = (me ^ 1) - 2 * way * hop
        return remote(
            shard(part, origin), shard(part, origin),
            pair_send.at[side, hop, part], pair_recv.at[side, hop, part], {"dp": me ^ 1},
        )

    def has(way, hop):
        behind = chip >= hop if way > 0 else chip < chips - hop
        ahead = chip < chips - 1 if way > 0 else chip >= 1
        return behind, ahead

    for part in (0, 1):
        for way in (1, -1):
            @pl.when(has(way, 0)[1])
            def _(way=way, part=part):
                along(way, 0, part).start()
    for part in (0, 1):
        across(1, 0, part).start()

    def forward(hop, part):
        for way in (1, -1):
            behind, ahead = has(way, hop + 1)

            @pl.when(behind)
            def _(way=way):
                arriving(way, hop, part).wait_recv()

            @pl.when(jnp.logical_and(behind, ahead))
            def _(way=way):
                along(way, hop + 1, part).start()

            @pl.when(behind)
            def _(way=way):
                across(way, hop + 1, part).start()

    def crossed(hop, part):
        if hop == 0:
            across_arriving(1, 0, part).wait_recv()
            return
        for way in (1, -1):
            @pl.when(has(way, hop)[0])
            def _(way=way):
                across_arriving(way, hop, part).wait_recv()

    lane = lax.broadcasted_iota(jnp.int32, (slots, 128), 1)

    def chosen(d):
        column = jnp.transpose(jnp.broadcast_to(all_ids[d], (128, slots)))
        return jnp.concatenate(
            [jnp.where(column == lane + c * 128, 1.0, 0.0).astype(bf16) for c in range(pool_rows // 128)], axis=1
        )

    own_cols = block(me_e, width)
    loads[3].wait()
    for d in peers_e:
        id_copies[d].wait_recv()
        stage_x[d - 1] = dot(chosen(d), tokens[...]).astype(bf16)
        send(stage_x.at[d - 1], routed.at[:, own_cols], tok_send.at[d, 0], tok_recv.at[d, 0], {"expert": me_e ^ d})
    loads[4].wait()
    for d in peers_e:
        stage_c[d - 1] = dot(chosen(d), cot[...]).astype(bf16)
        send(stage_c.at[d - 1], cot_rows.at[:, own_cols], tok_send.at[d, 1], tok_recv.at[d, 1], {"expert": me_e ^ d})

    last_hop = chips - 1
    forward(0, 0)
    choice = chosen(0)
    routed[:, own_cols] = dot(choice, tokens[...]).astype(bf16)
    cot_rows[:, own_cols] = dot(choice, cot[...]).astype(bf16)
    forward(0, 1)

    route_column = jnp.transpose(jnp.broadcast_to(route[...], (128, slots)))

    def tokens_in(d, part):
        land = (routed, cot_rows)[part]
        theirs = block(me_e ^ d, width)
        stage = (stage_x, stage_c)[part]
        remote(
            stage.at[d - 1], land.at[:, theirs], tok_send.at[d, part], tok_recv.at[d, part], {"expert": me_e ^ d}
        ).wait_recv()

    def turn(d):
        e = me_e ^ d
        per = width // rows_gu
        flipped = jnp.transpose(routed[:, block(e, width)])
        for i in range(per):
            at = block(e * (per // 2) + i // 2, rows_gu)
            x_t[(i % 2) ^ core, at, :] = flipped[i * rows_gu : (i + 1) * rows_gu]

    def scale(d):
        for c in range(width // 128):
            at = pl.ds(pl.multiple_of((me_e ^ d) * width + c * 128, 128), 128)
            cot_rows[:, at] = (route_column * cot_rows[:, at].astype(f32)).astype(bf16)

    tall = min(256, slots)

    def multiply(origin, first):
        at = block(origin, 2 * rows_gu)
        for m in range(slots // tall):
            part = dot(routed[m * tall : (m + 1) * tall, at], gu_full[at, :])
            if first:
                pre[m * tall : (m + 1) * tall, :] = part
            else:
                pre[m * tall : (m + 1) * tall, :] += part

    def multiply_hop(hop):
        crossed(hop, 0)
        for way in (1, -1):
            @pl.when(has(way, hop)[0])
            def _(way=way):
                multiply(chip - way * hop, False)

    turn(0)
    scale(0)
    for d in peers_e:
        tokens_in(d, 0)
        turn(d)
    crossed(0, 0)
    multiply(chip, True)
    for hop in range(1, chips):
        if hop > 1:
            forward(hop - 1, 0)
        multiply_hop(hop)
        if 1 < hop < last_hop:
            forward(hop - 1, 1)

    step = 16

    def activate(i, carry):
        at = pl.ds(pl.multiple_of(i * step, step), step)
        gate_pre, up_pre = pre[at, :hid], pre[at, hid:]
        sig = jax.nn.sigmoid(gate_pre)
        act = gate_pre * sig
        hidden[at, :] = (act * up_pre).astype(bf16)
        pre[at, :hid] = up_pre * sig * (1.0 + gate_pre * (1.0 - sig))
        pre[at, hid:] = act
        return carry

    lax.fori_loop(0, slots // step, activate, 0, unroll=2)
    flipped = jnp.transpose(hidden[...])
    for p in range(n_dp):
        h_t[(p % 2) ^ core, (p // 2) * rows_dn : (p // 2 + 1) * rows_dn, :] = flipped[p * rows_dn : (p + 1) * rows_dn]
    for d in peers_e:
        tokens_in(d, 1)
        scale(d)

    offset = [(2 << t) - 2 - t for t in range(tiers)]
    flying, news, totals = {}, {}, {}

    def blocks_at(t):
        return n_dp >> (t + 1)

    def launch(m, t, k):
        size = blocks_at(t) // chunks_of(blocks_at(t)) * rows[m]
        at = pl.ds(k * size, size)
        src = sent[m] if t == 0 else outs[m][t - 1]
        flying[m, t, k] = send(
            src.at[at], ins[m][t].at[at], blk_send.at[m, t, k], blk_recv.at[m, t, k], {"dp": me ^ (1 << t)}
        )

    def launch_all(m, t):
        for k in range(chunks_of(blocks_at(t))):
            launch(m, t, k)

    def gradient(m, away):
        left = h_t if m == DOWN else x_t
        total = half * rows[m]
        tile = min(256, total)
        parts = chunks_of(half)
        done = 0
        for i in range(total // tile):
            at = pl.ds(i * tile, tile)
            for c in range(0, cols[m], 512):
                if m == DOWN:
                    right = cot_rows[:, c : c + 512]
                else:
                    right = both[:, m * hid + c : m * hid + c + min(512, hid)]
                value = dot(left[1 if away else 0, at, :], right) * (1.0 / slots)
                to = pl.ds(c, value.shape[1])
                if away:
                    sent[m][at, to] = value.astype(bf16)
                else:
                    own[m][at, to] = value
            while away and done < parts and (i + 1) * tile >= (done + 1) * (total // parts):
                launch(m, 0, done)
                done += 1

    def low(t):
        return lax.shift_right_logical(me, 1) & ((1 << t) - 1)

    def bit_of(t):
        return lax.shift_right_logical(me, t) & 1

    def fold(x):
        return x[:8] + x[8:]

    def measure(m, t):
        blocks, steps = blocks_at(t), rows[m] // step
        parts = chunks_of(blocks)
        bit, base = bit_of(t), low(t)
        acc = tuple(jnp.zeros((8, lump), f32) for _ in range(3))

        def body(i, acc):
            j, r = i // steps, i % steps
            at_mine = pl.ds(pl.multiple_of(((j << t) + base) * rows[m] + r * step, step), step)
            at_other = pl.ds(pl.multiple_of(i * step, step), step)
            ab, aa, bb = acc
            for c in range(0, cols[m], lump):
                a = own[m][at_mine, c : c + lump]
                b = ins[m][t][at_other, c : c + lump].astype(f32)
                ab, aa, bb = ab + fold(a * b), aa + fold(a * a), bb + fold(b * b)
            return ab, aa, bb

        per = blocks // parts * steps
        for k in range(parts):
            flying[m, t, k].wait_recv()
            acc = lax.fori_loop(k * per, (k + 1) * per, body, acc, unroll=2 if per % 2 == 0 else 1)

        def lanes(x):
            total = x[:, :128]
            for c in range(1, lump // 128):
                total = total + x[:, c * 128 : (c + 1) * 128]
            return jnp.sum(total, axis=0, keepdims=True)

        ab, aa, bb = (lanes(x) for x in acc)
        local = jnp.concatenate(
            [ab, jnp.where(bit == 0, aa, bb), jnp.where(bit == 0, bb, aa), jnp.zeros((5, 128), f32)], axis=0
        )
        stats[m, t] = local
        totals[m, t] = local
        news[m, t] = [
            send(
                stats.at[m, t], stats_in.at[m, offset[t] + d - 1],
                st_send.at[m, offset[t] + d - 1], st_recv.at[m, offset[t] + d - 1], {"dp": me ^ d},
            )
            for d in range(1, 2 << t)
        ]

    def settle(m, t):
        total = totals[m, t]
        for d in range(1, 2 << t):
            news[m, t][d - 1].wait_recv()
            total = total + stats_in[m, offset[t] + d - 1]
        whole = jnp.sum(total, axis=1, keepdims=True)
        inner, bit = whole[0:1], bit_of(t)
        c_left, c_right = coefs(inner, whole[1:2]), coefs(inner, whole[2:3])
        c_mine = jnp.where(bit == 0, c_left, c_right)
        c_other = jnp.where(bit == 0, c_right, c_left)
        return jnp.broadcast_to(c_mine, (1, lump)), jnp.broadcast_to(c_other, (1, lump))

    def combine(m, t, c_m, c_o, count, which, store):
        steps, base = rows[m] // step, low(t)

        def body(i, carry):
            jj, r = i // steps, i % steps
            j = which(jj)
            at_mine = pl.ds(pl.multiple_of(((j << t) + base) * rows[m] + r * step, step), step)
            at_other = pl.ds(pl.multiple_of(j * rows[m] + r * step, step), step)
            for c in range(0, cols[m], lump):
                value = own[m][at_mine, c : c + lump] * c_m
                value = value + ins[m][t][at_other, c : c + lump].astype(f32) * c_o
                store(i, at_mine, pl.ds(c, lump), value)
            return carry

        n = count * steps
        lax.fori_loop(0, n, body, 0, unroll=2 if n % 2 == 0 else 1)

    def merge(m, t, hold=False):
        c_m, c_o = settle(m, t)
        up = bit_of(t + 1)
        count = blocks_at(t + 1)

        def store_away(i, at, to, value):
            outs[m][t][pl.ds(pl.multiple_of(i * step, step), step), to] = value.astype(bf16)

        def store_own(i, at, to, value):
            own[m][at, to] = value

        combine(m, t, c_m, c_o, count, lambda j: 2 * j + 1 - up, store_away)
        if not hold:
            launch_all(m, t + 1)
        combine(m, t, c_m, c_o, count, lambda j: 2 * j + up, store_own)

    weights_out = (new_gate_h, new_up_h, new_down_h)
    moments_out = (next_gate_h, next_up_h, next_down_h)
    stores = []

    def put(src, dst):
        copy = pltpu.make_async_copy(src, dst, out_sem.at[len(stores)])
        copy.start()
        stores.append(copy)

    def finish(m):
        t = tiers - 1
        c_m, c_o = settle(m, t)
        loads[5 + m].wait()

        def store(i, at, to, value):
            row = pl.ds(pl.multiple_of(i * step, step), step)
            following = momentum_decay * moments[m][row, to] + value
            moments[m][row, to] = following
            weights[m][row, to] = weights[m][row, to] - learning_rate * following

        combine(m, t, c_m, c_o, 1, lambda j: j, store)
        put(moments[m], moments_out[m].at[0])
        put(weights[m], weights_out[m].at[0])

    gradient(DOWN, True)
    gradient(DOWN, False)
    forward(last_hop - 1, 1)
    measure(DOWN, 0)

    for hop in range(chips):
        crossed(hop, 1)
    for m in range(slots // tall):
        at = slice(m * tall, (m + 1) * tall)
        back = dot_t(cot_rows[at, :], dn_full[...])
        both[at, :hid] = (back * pre[at, :hid]).astype(bf16)
        both[at, hid:] = (back * pre[at, hid:]).astype(bf16)
    merge(DOWN, 0)

    def slot_back(d):
        weight = gu_full[block(me_e ^ d, width), :]
        value = dot_t(both[...], weight).astype(bf16)
        if d == 0:
            returned[0:slots, :] = value
            return None
        slot_grad[d - 1] = value
        return send(
            slot_grad.at[d - 1], returned.at[pl.ds(d * slots, slots)], ret_send.at[d], ret_recv.at[d],
            {"expert": me_e ^ d},
        )

    def pool_sum():
        for copy in back_copies:
            copy.wait_recv()
        tile = 256

        @pl.loop(0, pool_rows // tile)
        def _(t):
            at = pl.multiple_of(t * tile, tile)
            row = lax.broadcasted_iota(jnp.int32, (tile, slots), 0) + at
            pick = jnp.concatenate(
                [jnp.where(row == all_ids[d], 1.0, 0.0).astype(bf16) for d in range(n_e)], axis=1
            )
            pool[pl.ds(at, tile), :] = dot(pick, returned[...])

        put(pool, pool_h)

    gradient(GATE, True)
    gradient(UP, True)
    gradient(GATE, False)
    measure(GATE, 0)
    gradient(UP, False)
    merge(GATE, 0)
    measure(UP, 0)
    back_copies = [slot_back(d) for d in peers_e]
    merge(UP, 0, hold=True)
    order = sorted(
        ((m, t) for m in range(3) for t in range(1, tiers)), key=lambda x: (2 * (x[1] - 1) + (x[0] + 1) % 3, -x[1])
    )
    for m, t in order:
        measure(m, t)
        if (m, t) == (DOWN, 1):
            slot_back(0)
        if t == tiers - 1:
            finish(m)
        else:
            merge(m, t)
        if (m, t) == (DOWN, 1):
            launch_all(UP, 1)
        if (m, t) == (DOWN, 2):
            pool_sum()

    for part in (0, 1):
        across(1, 0, part).wait_send()
    for hop in range(chips):
        for part in (0, 1):
            for way in (1, -1):
                behind, ahead = has(way, hop)

                @pl.when(jnp.logical_and(behind, ahead))
                def _(way=way, hop=hop, part=part):
                    along(way, hop, part).wait_send()

                if hop:
                    @pl.when(behind)
                    def _(way=way, hop=hop, part=part):
                        across(way, hop, part).wait_send()
    for copy in pending:
        copy.wait_send()
    for copy in stores:
        copy.wait()


def local(
    pool_tokens,
    pool_cotangent,
    token_ids,
    route_weights,
    gate_weight,
    up_weight,
    down_weight,
    momentum_gate,
    momentum_up,
    momentum_down,
):
    bf16, f32 = jnp.bfloat16, jnp.float32
    n_e, n_dp = lax.axis_size("expert"), lax.axis_size("dp")
    chips, half, tiers = n_dp // 2, n_dp // 2, n_dp.bit_length() - 1
    pool_rows, width = pool_tokens.shape
    slots = token_ids.shape[1]
    rows_gu, hid = gate_weight.shape[1:]
    rows_dn, full = down_weight.shape[1:]
    shapes = ((rows_gu, hid), (rows_gu, hid), (rows_dn, full))
    n_stats = sum((2 << t) - 1 for t in range(tiers))
    vmem, anywhere = pl.BlockSpec(memory_space=pltpu.VMEM), pl.BlockSpec(memory_space=pl.ANY)
    dma, buf = pltpu.SemaphoreType.DMA, pltpu.VMEM

    def per_matrix(blocks, kind):
        return [buf((blocks * r, c), kind) for r, c in shapes]

    def per_tier(first, kind):
        return [[buf(((n_dp >> (t + 1)) * r, c), kind) for t in range(first, tiers)] for r, c in shapes]

    like = [jax.ShapeDtypeStruct(x.shape, f32) for x in (gate_weight, up_weight, down_weight)]
    return pl.pallas_call(
        functools.partial(step_kernel, n_e, n_dp),
        out_shape=(*like, *like, jax.ShapeDtypeStruct((pool_rows, width), f32)),
        in_specs=[vmem] * 2 + [anywhere] * 8,
        out_specs=(anywhere,) * 7,
        scratch_shapes=[
            buf((pool_rows, width), bf16),
            buf((pool_rows, width), bf16),
            per_matrix(1, f32),
            per_matrix(1, f32),
            buf((n_e, 1, slots), jnp.int32),
            buf((n_e - 1, slots, width), bf16),
            buf((n_e - 1, slots, width), bf16),
            buf((slots, full), bf16),
            buf((slots, full), bf16),
            buf((n_dp * rows_gu, 2 * hid), bf16),
            buf((n_dp * rows_dn, full), bf16),
            buf((2, half * rows_gu, slots), bf16),
            buf((2, half * rows_dn, slots), bf16),
            buf((slots, hid), bf16),
            buf((slots, 2 * hid), f32),
            buf((slots, 2 * hid), bf16),
            buf((n_e - 1, slots, width), bf16),
            buf((n_e * slots, width), bf16),
            buf((pool_rows, width), f32),
            per_matrix(half, f32),
            per_matrix(half, bf16),
            per_tier(1, bf16),
            per_tier(0, bf16),
            buf((3, tiers, 8, 128), f32),
            buf((3, n_stats, 8, 128), f32),
            dma((8,)), dma((7,)), dma((n_e,)), dma((n_e,)), dma((n_e, 2)), dma((n_e, 2)),
            dma((2, chips, 2)), dma((2, chips, 2)), dma((2, chips, 2)), dma((2, chips, 2)),
            dma((n_e,)), dma((n_e,)), dma((3, tiers, 2)), dma((3, tiers, 2)), dma((3, n_stats)), dma((3, n_stats)),
        ],
        compiler_params=pltpu.CompilerParams(
            collective_id=1, has_side_effects=True, vmem_limit_bytes=63 * 1024 * 1024
        ),
    )(
        token_ids, route_weights, pool_tokens, pool_cotangent, gate_weight, up_weight, down_weight,
        momentum_gate, momentum_up, momentum_down,
    )


def solution(mesh):
    in_specs = (
        P("dp", "expert"),
        P("dp", "expert"),
        P("expert", "dp"),
        P("expert", "dp"),
        P("expert", "dp", None),
        P("expert", "dp", None),
        P("expert", "dp", None),
        P("expert", "dp", None),
        P("expert", "dp", None),
        P("expert", "dp", None),
    )
    out_specs = (
        P("expert", "dp", None),
        P("expert", "dp", None),
        P("expert", "dp", None),
        P("expert", "dp", None),
        P("expert", "dp", None),
        P("expert", "dp", None),
        P("dp", "expert"),
    )
    return jax.shard_map(local, mesh=mesh, in_specs=in_specs, out_specs=out_specs, check_vma=False)
```

time: 197 us -> 165 us (0.84)
  matrix products: 20.1 us -> 0 us
  Pallas kernels: 164 us -> 152 us
  local copies, waits for them, and re-layouts: 2.57 us -> 12.3 us
  other arithmetic: 8.92 us -> 0 us
    dot_general x5 -> x0, matrix products: 20.1 us -> none  [dot(): lax.dot_general(left, right, ((dims[0], dims[1]), ((), ())), preferred_el...]
    pallas_call x2 -> x1, Pallas kernels: 164 us -> 152 us  [local(): pl.pallas_call(functools.partial(step_kernel, n_e, n_dp), out_shape=(*lik...]
    unnamed x25 -> x11, local copies, waits for them, and re-layouts: 2.57 us -> 12.3 us
    broadcast_in_dim x2 -> x0, other arithmetic: 4.97 us -> none  [the longest x1 2.84 us: local(): next_up[None]]
where the time goes in v1:
time: 165 us
  Pallas kernels  152 us (92%)
  local copies, waits for them, and re-layouts  12.3 us (7%)
    pallas_call x1, Pallas kernels, local(): pl.pallas_call(functools.partial(step_kernel, n_e, n_dp), out_shape=(*lik...  152 us
    unnamed x11, local copies, waits for them, and re-layouts  12.3 us

profile of v1, /device:TPU:0, one launch (start us, length us, event | category | flops | bytes accessed | tf_op | source)
XLA Modules:
  0.0 164.7 jit_solution(6468020055568348050)
XLA Ops:
  0.6 151.7 %shard_map.153 = (f32[1,256,512]{2,1,0:T(8,128)}, f32[1,256,512]{2,1,0:T(8,128)}, f32[1,64,2048]{2,1,0:T(8,128)}, f32[1,256,512]{2,1,0:T(8,128)}, f32[1,256,512]...) custom-call(s32[1,512]{1,0:T(1,128)} %ids.1, f32[1,512]{1,0:T(1,128)} %route.1, bf16[2048,512]{1,0:T(8,128)(2,1)} %tok_h.1, ...), custom_call_target="tpu_custom_call" | custom-call | tf_op jit(solution)/shard_map/pallas_call | solution.py:563
  152.3 0.0 copy-start.1
  152.3 0.0 copy-start
  152.4 2.0 %copy.24 = f32[1,256,512]{2,1,0:T(8,128)} copy(f32[1,256,512]{2,1,0:T(8,128)} %get-tuple-element.14) | data formatting | bytes 1048576
  154.4 1.9 %copy.25 = f32[1,256,512]{2,1,0:T(8,128)} copy(f32[1,256,512]{2,1,0:T(8,128)} %get-tuple-element.15) | data formatting | bytes 1048576
  156.2 1.9 %copy.26 = f32[1,64,2048]{2,1,0:T(8,128)} copy(f32[1,64,2048]{2,1,0:T(8,128)} %get-tuple-element.16) | data formatting | bytes 1048576
  158.1 1.9 %copy.27 = f32[1,256,512]{2,1,0:T(8,128)} copy(f32[1,256,512]{2,1,0:T(8,128)} %get-tuple-element.17) | data formatting | bytes 1048576
  160.0 1.9 %copy.28 = f32[1,256,512]{2,1,0:T(8,128)} copy(f32[1,256,512]{2,1,0:T(8,128)} %get-tuple-element.18) | data formatting | bytes 1048576
  161.9 0.0 copy-done.1
  161.9 0.8 copy.29
  162.6 0.0 copy-done
  162.7 2.0 %copy.30 = f32[2048,512]{1,0:T(8,128)} copy(f32[2048,512]{1,0:T(8,128)S(1)} %copy-done) | data formatting | bytes 8388608
Async XLA Ops:
  152.3 9.5 %copy-start.1 = (f32[1,64,2048]{2,1,0:T(8,128)S(1)}, f32[1,64,2048]{2,1,0:T(8,128)}, u32[]{:S(2)}) copy-start(f32[1,64,2048]{2,1,0:T(8,128)} %get-tuple-element.19) | copy-start | bytes 1572868
  152.3 10.3 %copy-start = (f32[2048,512]{1,0:T(8,128)S(1)}, f32[2048,512]{1,0:T(8,128)}, u32[]{:S(2)}) copy-start(f32[2048,512]{1,0:T(8,128)} %get-tuple-element.20) | copy-start | bytes 12582916

commit v2 on v1

--- a/solution.py
+++ b/solution.py
@@ -25,11 +25,11 @@
 def step_kernel(
     n_e, n_dp,
     ids, route, tok_h, cot_h, gate_h, up_h, down_h, mom_gate_h, mom_up_h, mom_down_h,
-    new_gate_h, new_up_h, new_down_h, next_gate_h, next_up_h, next_down_h, pool_h,
+    new_gate, new_up, new_down, next_gate, next_up, next_down, pool,
     tokens, cot, weights, moments, all_ids, stage_x, stage_c, routed, cot_rows,
-    gu_full, dn_full, x_t, h_t, hidden, pre, both, slot_grad, returned, pool,
+    gu_full, dn_full, x_t, h_t, hidden, pre, both, slot_grad, returned,
     own, sent, outs, ins, stats, stats_in,
-    in_sem, out_sem, id_send, id_recv, tok_send, tok_recv, line_send, line_recv, pair_send, pair_recv,
+    in_sem, id_send, id_recv, tok_send, tok_recv, line_send, line_recv, pair_send, pair_recv,
     ret_send, ret_recv, blk_send, blk_recv, st_send, st_recv,
 ):
     f32, bf16 = jnp.float32, jnp.bfloat16
@@ -286,17 +286,24 @@
     def blocks_at(t):
         return n_dp >> (t + 1)
 
-    def launch(m, t, k):
+    def block_copy(m, t, k):
         size = blocks_at(t) // chunks_of(blocks_at(t)) * rows[m]
         at = pl.ds(k * size, size)
         src = sent[m] if t == 0 else outs[m][t - 1]
-        flying[m, t, k] = send(
+        return remote(
             src.at[at], ins[m][t].at[at], blk_send.at[m, t, k], blk_recv.at[m, t, k], {"dp": me ^ (1 << t)}
         )
 
-    def launch_all(m, t):
+    def launch_all(m, t, now=None):
         for k in range(chunks_of(blocks_at(t))):
-            launch(m, t, k)
+            copy = block_copy(m, t, k)
+            if now is None:
+                copy.start()
+            else:
+                pl.when(now)(copy.start)
+            if (m, t, k) not in flying:
+                flying[m, t, k] = copy
+                pending.append(copy)
 
     def gradient(m, away):
         left = h_t if m == DOWN else x_t
@@ -318,7 +325,9 @@
                 else:
                     own[m][at, to] = value
             while away and done < parts and (i + 1) * tile >= (done + 1) * (total // parts):
-                launch(m, 0, done)
+                flying[m, 0, done] = block_copy(m, 0, done)
+                flying[m, 0, done].start()
+                pending.append(flying[m, 0, done])
                 done += 1
 
     def low(t):
@@ -401,7 +410,7 @@
         n = count * steps
         lax.fori_loop(0, n, body, 0, unroll=2 if n % 2 == 0 else 1)
 
-    def merge(m, t, hold=False):
+    def merge(m, t):
         c_m, c_o = settle(m, t)
         up = bit_of(t + 1)
         count = blocks_at(t + 1)
@@ -413,18 +422,9 @@
             own[m][at, to] = value
 
         combine(m, t, c_m, c_o, count, lambda j: 2 * j + 1 - up, store_away)
-        if not hold:
-            launch_all(m, t + 1)
         combine(m, t, c_m, c_o, count, lambda j: 2 * j + up, store_own)
 
-    weights_out = (new_gate_h, new_up_h, new_down_h)
-    moments_out = (next_gate_h, next_up_h, next_down_h)
-    stores = []
-
-    def put(src, dst):
-        copy = pltpu.make_async_copy(src, dst, out_sem.at[len(stores)])
-        copy.start()
-        stores.append(copy)
+    new, following = (new_gate, new_up, new_down), (next_gate, next_up, next_down)
 
     def finish(m):
         t = tiers - 1
@@ -433,13 +433,11 @@
 
         def store(i, at, to, value):
             row = pl.ds(pl.multiple_of(i * step, step), step)
-            following = momentum_decay * moments[m][row, to] + value
-            moments[m][row, to] = following
-            weights[m][row, to] = weights[m][row, to] - learning_rate * following
+            momentum = momentum_decay * moments[m][row, to] + value
+            following[m][0, row, to] = momentum
+            new[m][0, row, to] = weights[m][row, to] - learning_rate * momentum
 
         combine(m, t, c_m, c_o, 1, lambda j: j, store)
-        put(moments[m], moments_out[m].at[0])
-        put(weights[m], weights_out[m].at[0])
 
     gradient(DOWN, True)
     gradient(DOWN, False)
@@ -481,8 +479,7 @@
             )
             pool[pl.ds(at, tile), :] = dot(pick, returned[...])
 
-        put(pool, pool_h)
-
+    launch_all(DOWN, 1)
     gradient(GATE, True)
     gradient(UP, True)
     gradient(GATE, False)
@@ -491,22 +488,31 @@
     merge(GATE, 0)
     measure(UP, 0)
     back_copies = [slot_back(d) for d in peers_e]
-    merge(UP, 0, hold=True)
-    order = sorted(
-        ((m, t) for m in range(3) for t in range(1, tiers)), key=lambda x: (2 * (x[1] - 1) + (x[0] + 1) % 3, -x[1])
-    )
-    for m, t in order:
-        measure(m, t)
-        if (m, t) == (DOWN, 1):
-            slot_back(0)
-        if t == tiers - 1:
-            finish(m)
-        else:
-            merge(m, t)
-        if (m, t) == (DOWN, 1):
-            launch_all(UP, 1)
-        if (m, t) == (DOWN, 2):
-            pool_sum()
+    merge(UP, 0)
+    same_way = bit_of(1) == bit_of(2)
+    measure(DOWN, 1)
+    launch_all(GATE, 1)
+    slot_back(0)
+    merge(DOWN, 1)
+    launch_all(DOWN, 2, jnp.logical_not(same_way))
+    measure(GATE, 1)
+    launch_all(DOWN, 2, same_way)
+    launch_all(UP, 1)
+    merge(GATE, 1)
+    launch_all(GATE, 2, jnp.logical_not(same_way))
+    pool_sum()
+    measure(UP, 1)
+    launch_all(GATE, 2, same_way)
+    merge(UP, 1)
+    launch_all(UP, 2)
+    for t in range(2, tiers):
+        for m in (DOWN, GATE, UP):
+            measure(m, t)
+            if t == tiers - 1:
+                finish(m)
+            else:
+                merge(m, t)
+                launch_all(m, t + 1)
 
     for part in (0, 1):
         across(1, 0, part).wait_send()
@@ -525,7 +531,15 @@
                         across(way, hop, part).wait_send()
     for copy in pending:
         copy.wait_send()
-    for copy in stores:
+
+
+def store_kernel(*refs):
+    *pairs, sem = refs
+    count = len(pairs) // 2
+    copies = [pltpu.make_async_copy(pairs[i], pairs[count + i], sem.at[i]) for i in range(count)]
+    for copy in copies:
+        copy.start()
+    for copy in copies:
         copy.wait()
 
 
@@ -559,12 +573,13 @@
     def per_tier(first, kind):
         return [[buf(((n_dp >> (t + 1)) * r, c), kind) for t in range(first, tiers)] for r, c in shapes]
 
-    like = [jax.ShapeDtypeStruct(x.shape, f32) for x in (gate_weight, up_weight, down_weight)]
-    return pl.pallas_call(
+    like = [(x.shape, f32) for x in (gate_weight, up_weight, down_weight)]
+    like = [*like, *like, ((pool_rows, width), f32)]
+    results = pl.pallas_call(
         functools.partial(step_kernel, n_e, n_dp),
-        out_shape=(*like, *like, jax.ShapeDtypeStruct((pool_rows, width), f32)),
+        out_shape=[buf(*x) for x in like],
         in_specs=[vmem] * 2 + [anywhere] * 8,
-        out_specs=(anywhere,) * 7,
+        out_specs=[vmem] * len(like),
         scratch_shapes=[
             buf((pool_rows, width), bf16),
             buf((pool_rows, width), bf16),
@@ -584,24 +599,31 @@
             buf((slots, 2 * hid), bf16),
             buf((n_e - 1, slots, width), bf16),
             buf((n_e * slots, width), bf16),
-            buf((pool_rows, width), f32),
             per_matrix(half, f32),
             per_matrix(half, bf16),
             per_tier(1, bf16),
             per_tier(0, bf16),
             buf((3, tiers, 8, 128), f32),
             buf((3, n_stats, 8, 128), f32),
-            dma((8,)), dma((7,)), dma((n_e,)), dma((n_e,)), dma((n_e, 2)), dma((n_e, 2)),
+            dma((8,)), dma((n_e,)), dma((n_e,)), dma((n_e, 2)), dma((n_e, 2)),
             dma((2, chips, 2)), dma((2, chips, 2)), dma((2, chips, 2)), dma((2, chips, 2)),
             dma((n_e,)), dma((n_e,)), dma((3, tiers, 2)), dma((3, tiers, 2)), dma((3, n_stats)), dma((3, n_stats)),
         ],
         compiler_params=pltpu.CompilerParams(
-            collective_id=1, has_side_effects=True, vmem_limit_bytes=63 * 1024 * 1024
+            collective_id=1, has_side_effects=True, vmem_limit_bytes=54 * 1024 * 1024
         ),
     )(
         token_ids, route_weights, pool_tokens, pool_cotangent, gate_weight, up_weight, down_weight,
         momentum_gate, momentum_up, momentum_down,
     )
+    return pl.pallas_call(
+        store_kernel,
+        out_shape=[jax.ShapeDtypeStruct(*x) for x in like],
+        in_specs=[vmem] * len(like),
+        out_specs=[anywhere] * len(like),
+        scratch_shapes=[dma((len(like),))],
+        compiler_params=pltpu.CompilerParams(vmem_limit_bytes=1024 * 1024),
+    )(*results)
 
 
 def solution(mesh):

time: 165 us -> 146 us (0.88)
  local copies, waits for them, and re-layouts: 12.3 us -> 0 us
  Pallas kernels: 152 us -> 145 us
    unnamed x11 -> x0, local copies, waits for them, and re-layouts: 12.3 us -> none
    pallas_call x1 -> x2, Pallas kernels: 152 us -> 145 us  [the longest x1 142 us: local(): pl.pallas_call(functools.partial(step_kernel, n_e, n_dp), out_shape=[buf(...]
where the time goes in v2:
time: 146 us
  Pallas kernels  145 us (99%)
    pallas_call x1, Pallas kernels, local(): pl.pallas_call(functools.partial(step_kernel, n_e, n_dp), out_shape=[buf(...  142 us
    pallas_call x1, Pallas kernels, local(): pl.pallas_call(store_kernel, out_shape=[jax.ShapeDtypeStruct(*x) for x in...  3.11 us

profile of v2, /device:TPU:0, one launch (start us, length us, event | category | flops | bytes accessed | tf_op | source)
XLA Modules:
  0.0 145.6 jit_solution(9768870031349843190)
XLA Ops:
  0.6 141.7 %shard_map.153 = (f32[1,256,512]{2,1,0:T(8,128)S(1)}, f32[1,256,512]{2,1,0:T(8,128)S(1)}, f32[1,64,2048]{2,1,0:T(8,128)S(1)}, f32[1,256,512]{2,1,0:T(8,128)S(1)}...) custom-call(s32[1,512]{1,0:T(1,128)} %ids.1, f32[1,512]{1,0:T(1,128)} %route.1, ...), custom_call_target="tpu_custom_call" | custom-call | tf_op jit(solution)/shard_map/pallas_call | solution.py:578
  142.3 3.1 %shard_map.154 = (f32[1,256,512]{2,1,0:T(8,128)}, f32[1,256,512]{2,1,0:T(8,128)}, f32[1,64,2048]{2,1,0:T(8,128)}, f32[1,256,512]{2,1,0:T(8,128)}, f32[1,256,512]...) custom-call(f32[1,256,512]{2,1,0:T(8,128)S(1)} %get-tuple-element.14.refs_0_, ...), custom_call_target="tpu_custom_call" | custom-call | tf_op jit(solution)/shard_map/pallas_call | solution.py:619

commit v3 on v2

--- a/solution.py
+++ b/solution.py
@@ -28,9 +28,10 @@
     new_gate, new_up, new_down, next_gate, next_up, next_down, pool,
     tokens, cot, weights, moments, all_ids, stage_x, stage_c, routed, cot_rows,
     gu_full, dn_full, x_t, h_t, hidden, pre, both, slot_grad, returned,
-    own, sent, outs, ins, stats, stats_in,
+    own, sent, outs, ins, stats, stats_in, far_out, far_in, far_stats, far_stats_in,
     in_sem, id_send, id_recv, tok_send, tok_recv, line_send, line_recv, pair_send, pair_recv,
-    ret_send, ret_recv, blk_send, blk_recv, st_send, st_recv,
+    ret_send, ret_recv, blk_send, blk_recv, st_send, st_recv, dn_send, dn_recv,
+    far_send, far_recv, table_send, table_recv,
 ):
     f32, bf16 = jnp.float32, jnp.bfloat16
     MESH = pl.DeviceIdType.MESH
@@ -276,9 +277,6 @@
     flipped = jnp.transpose(hidden[...])
     for p in range(n_dp):
         h_t[(p % 2) ^ core, (p // 2) * rows_dn : (p // 2 + 1) * rows_dn, :] = flipped[p * rows_dn : (p + 1) * rows_dn]
-    for d in peers_e:
-        tokens_in(d, 1)
-        scale(d)
 
     offset = [(2 << t) - 2 - t for t in range(tiers)]
     flying, news, totals = {}, {}, {}
@@ -306,30 +304,33 @@
                 pending.append(copy)
 
     def gradient(m, away):
-        left = h_t if m == DOWN else x_t
         total = half * rows[m]
         tile = min(256, total)
         parts = chunks_of(half)
         done = 0
         for i in range(total // tile):
             at = pl.ds(i * tile, tile)
-            for c in range(0, cols[m], 512):
-                if m == DOWN:
-                    right = cot_rows[:, c : c + 512]
-                else:
-                    right = both[:, m * hid + c : m * hid + c + min(512, hid)]
-                value = dot(left[1 if away else 0, at, :], right) * (1.0 / slots)
-                to = pl.ds(c, value.shape[1])
-                if away:
-                    sent[m][at, to] = value.astype(bf16)
-                else:
-                    own[m][at, to] = value
+            value = dot(x_t[1 if away else 0, at, :], both[:, m * hid : (m + 1) * hid]) * (1.0 / slots)
+            if away:
+                sent[m][at, :] = value.astype(bf16)
+            else:
+                own[m][at, :] = value
             while away and done < parts and (i + 1) * tile >= (done + 1) * (total // parts):
                 flying[m, 0, done] = block_copy(m, 0, done)
                 flying[m, 0, done].start()
                 pending.append(flying[m, 0, done])
                 done += 1
 
+    down_copies = {}
+
+    def gradient_down(d):
+        at = block(me_e ^ d, width)
+        sent[DOWN][:, at] = (dot(h_t[1], cot_rows[:, at]) * (1.0 / slots)).astype(bf16)
+        down_copies[d] = send(
+            sent[DOWN].at[:, at], ins[DOWN][0].at[:, at], dn_send.at[d], dn_recv.at[d], {"dp": me ^ 1}
+        )
+        own[DOWN][:, at] = dot(h_t[0], cot_rows[:, at]) * (1.0 / slots)
+
     def low(t):
         return lax.shift_right_logical(me, 1) & ((1 << t) - 1)
 
@@ -338,6 +339,12 @@
 
     def fold(x):
         return x[:8] + x[8:]
+
+    def lanes(x):
+        total = x[:, :128]
+        for c in range(1, x.shape[1] // 128):
+            total = total + x[:, c * 128 : (c + 1) * 128]
+        return jnp.sum(total, axis=0, keepdims=True)
 
     def measure(m, t):
         blocks, steps = blocks_at(t), rows[m] // step
@@ -345,27 +352,31 @@
         bit, base = bit_of(t), low(t)
         acc = tuple(jnp.zeros((8, lump), f32) for _ in range(3))
 
-        def body(i, acc):
+        def body(places, i, acc):
             j, r = i // steps, i % steps
             at_mine = pl.ds(pl.multiple_of(((j << t) + base) * rows[m] + r * step, step), step)
             at_other = pl.ds(pl.multiple_of(i * step, step), step)
             ab, aa, bb = acc
-            for c in range(0, cols[m], lump):
-                a = own[m][at_mine, c : c + lump]
-                b = ins[m][t][at_other, c : c + lump].astype(f32)
+            for at in places:
+                a = own[m][at_mine, at]
+                b = ins[m][t][at_other, at].astype(f32)
                 ab, aa, bb = ab + fold(a * b), aa + fold(a * a), bb + fold(b * b)
             return ab, aa, bb
 
-        per = blocks // parts * steps
-        for k in range(parts):
-            flying[m, t, k].wait_recv()
-            acc = lax.fori_loop(k * per, (k + 1) * per, body, acc, unroll=2 if per % 2 == 0 else 1)
-
-        def lanes(x):
-            total = x[:, :128]
-            for c in range(1, lump // 128):
-                total = total + x[:, c * 128 : (c + 1) * 128]
-            return jnp.sum(total, axis=0, keepdims=True)
+        if m == DOWN and t == 0:
+            for d in (0, *peers_e):
+                down_copies[d].wait_recv()
+                first = (me_e ^ d) * width
+                places = [pl.ds(pl.multiple_of(first + c, lump), lump) for c in range(0, width, lump)]
+                acc = lax.fori_loop(0, blocks * steps, functools.partial(body, places), acc, unroll=2)
+        else:
+            per = blocks // parts * steps
+            places = [pl.ds(c, lump) for c in range(0, cols[m], lump)]
+            for k in range(parts):
+                flying[m, t, k].wait_recv()
+                acc = lax.fori_loop(
+                    k * per, (k + 1) * per, functools.partial(body, places), acc, unroll=2 if per % 2 == 0 else 1
+                )
 
         ab, aa, bb = (lanes(x) for x in acc)
         local = jnp.concatenate(
@@ -433,25 +444,136 @@
 
         def store(i, at, to, value):
             row = pl.ds(pl.multiple_of(i * step, step), step)
-            momentum = momentum_decay * moments[m][row, to] + value
-            following[m][0, row, to] = momentum
-            new[m][0, row, to] = weights[m][row, to] - learning_rate * momentum
+            update(m, row, to, value)
 
         combine(m, t, c_m, c_o, 1, lambda j: j, store)
 
-    gradient(DOWN, True)
-    gradient(DOWN, False)
+    def update(m, row, to, value):
+        momentum = momentum_decay * moments[m][row, to] + value
+        following[m][0, row, to] = momentum
+        new[m][0, row, to] = weights[m][row, to] - learning_rate * momentum
+
+    same_way = bit_of(1) == bit_of(2)
+    other_way = jnp.logical_not(same_way)
+
+    far = {}
+
+    def scatter(m):
+        c_m, c_o = settle(m, 0)
+        for r in (3, 2, 1):
+            def store_far(i, at, to, value, r=r):
+                far_out[pl.ds(pl.multiple_of((r - 1) * rows[m] + i * step, step), step), to] = value.astype(bf16)
+
+            combine(m, 0, c_m, c_o, 1, lambda j, r=r: chip ^ r, store_far)
+            at = pl.ds((r - 1) * rows[m], rows[m])
+            far[r] = remote(far_out.at[at], far_in.at[at], far_send.at[r - 1], far_recv.at[r - 1], {"dp": me ^ (2 * r)})
+            pending.append(far[r])
+            if r == 3:
+                far[r].start()
+            elif r == 2:
+                pl.when(other_way)(far[r].start)
+
+        def store_own(i, at, to, value):
+            own[m][at, to] = value
+
+        combine(m, 0, c_m, c_o, 1, lambda j: chip, store_own)
+
+    def by_chip(swap, items):
+        for b in (0, 1):
+            bit = lax.shift_right_logical(chip, b) & 1
+            items = {k: jnp.where(bit == 0, items[k], items[swap(k, 1 << b)]) for k in items}
+        return items
+
+    pairs4 = [(i, j) for i in range(4) for j in range(4)]
+
+    def far_tiles(m, i, to):
+        mine = pl.ds(pl.multiple_of(chip * rows[m] + i * step, step), step)
+        tiles = [own[m][mine, to]]
+        for r in (1, 2, 3):
+            tiles.append(far_in[pl.ds(pl.multiple_of((r - 1) * rows[m] + i * step, step), step), to].astype(f32))
+        return tiles
+
+    def gram(m):
+        for r in (1, 2, 3):
+            far[r].wait_recv()
+        wide = lump // 2
+        upper = [(i, j) for i, j in pairs4 if i <= j]
+
+        def body(i, acc):
+            for c in range(0, cols[m], wide):
+                v = far_tiles(m, i, pl.ds(c, wide))
+                acc = tuple(x + fold(v[a] * v[b]) for x, (a, b) in zip(acc, upper))
+            return acc
+
+        acc = lax.fori_loop(0, rows[m] // step, body, tuple(jnp.zeros((8, wide), f32) for _ in upper))
+        sums = {k: lanes(x) for k, x in zip(upper, acc)}
+        sums = {(i, j): sums[min(i, j), max(i, j)] for i, j in pairs4}
+        sums = by_chip(lambda k, s: (k[0] ^ s, k[1] ^ s), sums)
+        local = jnp.concatenate([sums[k] for k in pairs4], axis=0)
+        far_stats[...] = local
+        totals[m, 1] = local
+        news[m, 1] = [
+            send(far_stats, far_stats_in.at[d - 1], table_send.at[d - 1], table_recv.at[d - 1], {"dp": me ^ d})
+            for d in range(1, n_dp)
+        ]
+
+    def finish_far(m):
+        total = totals[m, 1]
+        for d in range(1, n_dp):
+            news[m, 1][d - 1].wait_recv()
+            total = total + far_stats_in[d - 1]
+        whole = jnp.sum(total, axis=1, keepdims=True)
+        g = {(i, j): whole[4 * i + j : 4 * i + j + 1] for i, j in pairs4}
+        share = {}
+        for a, b in ((0, 1), (2, 3)):
+            share[a], share[b] = coefs(g[a, b], g[a, a]), coefs(g[a, b], g[b, b])
+
+        def norm(a, b):
+            value = share[a] * share[a] * g[a, a] + 2.0 * share[a] * share[b] * g[a, b] + share[b] * share[b] * g[b, b]
+            return jnp.maximum(value, 0.0)
+
+        inner = sum(share[a] * share[b] * g[a, b] for a in (0, 1) for b in (2, 3))
+        c_left, c_right = coefs(inner, norm(0, 1)), coefs(inner, norm(2, 3))
+        w = {a: share[a] * (c_left if a < 2 else c_right) for a in range(4)}
+        w = by_chip(lambda k, s: k ^ s, w)
+        w = [jnp.broadcast_to(w[r], (1, lump)) for r in range(4)]
+        loads[5 + m].wait()
+
+        def body(i, carry):
+            row = pl.ds(pl.multiple_of(i * step, step), step)
+            for c in range(0, cols[m], lump):
+                to = pl.ds(c, lump)
+                v = far_tiles(m, i, to)
+                update(m, row, to, v[0] * w[0] + v[1] * w[1] + (v[2] * w[2] + v[3] * w[3]))
+            return carry
+
+        lax.fori_loop(0, rows[m] // step, body, 0, unroll=2)
+
+    gradient_down(0)
+    for d in peers_e:
+        tokens_in(d, 1)
+        scale(d)
+        gradient_down(d)
     forward(last_hop - 1, 1)
     measure(DOWN, 0)
-
     for hop in range(chips):
         crossed(hop, 1)
-    for m in range(slots // tall):
+
+    def backward(m):
         at = slice(m * tall, (m + 1) * tall)
         back = dot_t(cot_rows[at, :], dn_full[...])
         both[at, :hid] = (back * pre[at, :hid]).astype(bf16)
         both[at, hid:] = (back * pre[at, hid:]).astype(bf16)
-    merge(DOWN, 0)
+
+    backward(0)
+    straight = chips == 4
+    if straight:
+        scatter(DOWN)
+    else:
+        merge(DOWN, 0)
+        launch_all(DOWN, 1)
+    for m in range(1, slots // tall):
+        backward(m)
 
     def slot_back(d):
         weight = gu_full[block(me_e ^ d, width), :]
@@ -479,40 +601,57 @@
             )
             pool[pl.ds(at, tile), :] = dot(pick, returned[...])
 
-    launch_all(DOWN, 1)
     gradient(GATE, True)
     gradient(UP, True)
     gradient(GATE, False)
     measure(GATE, 0)
     gradient(UP, False)
     merge(GATE, 0)
+    if straight:
+        launch_all(GATE, 1)
+        pl.when(same_way)(far[2].start)
     measure(UP, 0)
     back_copies = [slot_back(d) for d in peers_e]
     merge(UP, 0)
-    same_way = bit_of(1) == bit_of(2)
-    measure(DOWN, 1)
-    launch_all(GATE, 1)
     slot_back(0)
-    merge(DOWN, 1)
-    launch_all(DOWN, 2, jnp.logical_not(same_way))
-    measure(GATE, 1)
-    launch_all(DOWN, 2, same_way)
-    launch_all(UP, 1)
-    merge(GATE, 1)
-    launch_all(GATE, 2, jnp.logical_not(same_way))
-    pool_sum()
-    measure(UP, 1)
-    launch_all(GATE, 2, same_way)
-    merge(UP, 1)
-    launch_all(UP, 2)
-    for t in range(2, tiers):
-        for m in (DOWN, GATE, UP):
-            measure(m, t)
-            if t == tiers - 1:
-                finish(m)
-            else:
-                merge(m, t)
-                launch_all(m, t + 1)
+    if straight:
+        measure(GATE, 1)
+        launch_all(UP, 1)
+        merge(GATE, 1)
+        launch_all(GATE, 2)
+        measure(UP, 1)
+        pl.when(other_way)(far[1].start)
+        measure(GATE, 2)
+        merge(UP, 1)
+        launch_all(UP, 2)
+        pl.when(same_way)(far[1].start)
+        pool_sum()
+        finish(GATE)
+        gram(DOWN)
+        measure(UP, 2)
+        finish_far(DOWN)
+        finish(UP)
+    else:
+        measure(DOWN, 1)
+        launch_all(GATE, 1)
+        merge(DOWN, 1)
+        measure(GATE, 1)
+        launch_all(DOWN, 2)
+        launch_all(UP, 1)
+        merge(GATE, 1)
+        pool_sum()
+        measure(UP, 1)
+        launch_all(GATE, 2)
+        merge(UP, 1)
+        launch_all(UP, 2)
+        for t in range(2, tiers):
+            for m in (DOWN, GATE, UP):
+                measure(m, t)
+                if t == tiers - 1:
+                    finish(m)
+                else:
+                    merge(m, t)
+                    launch_all(m, t + 1)
 
     for part in (0, 1):
         across(1, 0, part).wait_send()
@@ -605,9 +744,14 @@
             per_tier(0, bf16),
             buf((3, tiers, 8, 128), f32),
             buf((3, n_stats, 8, 128), f32),
+            buf((3 * rows_dn, full), bf16),
+            buf((3 * rows_dn, full), bf16),
+            buf((16, 128), f32),
+            buf((7, 16, 128), f32),
             dma((8,)), dma((n_e,)), dma((n_e,)), dma((n_e, 2)), dma((n_e, 2)),
             dma((2, chips, 2)), dma((2, chips, 2)), dma((2, chips, 2)), dma((2, chips, 2)),
-            dma((n_e,)), dma((n_e,)), dma((3, tiers, 2)), dma((3, tiers, 2)), dma((3, n_stats)), dma((3, n_stats)),
+            dma((n_e,)), dma((n_e,)), dma((3, tiers, 2)), dma((3, tiers, 2)), dma((3, n_stats)), dma((3, n_stats)), dma((n_e,)), dma((n_e,)),
+            dma((3,)), dma((3,)), dma((7,)), dma((7,)),
         ],
         compiler_params=pltpu.CompilerParams(
             collective_id=1, has_side_effects=True, vmem_limit_bytes=54 * 1024 * 1024

time: 146 us -> 132 us (0.904)
  Pallas kernels: 145 us -> 131 us
    pallas_call x1, Pallas kernels: 142 us -> 128 us  [local(): pl.pallas_call(functools.partial(step_kernel, n_e, n_dp), out_shape=[buf(...]
where the time goes in v3:
time: 132 us
  Pallas kernels  131 us (99%)
    pallas_call x1, Pallas kernels, local(): pl.pallas_call(functools.partial(step_kernel, n_e, n_dp), out_shape=[buf(...  128 us
    pallas_call x1, Pallas kernels, local(): pl.pallas_call(store_kernel, out_shape=[jax.ShapeDtypeStruct(*x) for x in...  3.11 us

profile of v3, /device:TPU:0, one launch (start us, length us, event | category | flops | bytes accessed | tf_op | source)
XLA Modules:
  0.0 131.7 jit_solution(9335803625667860877)
XLA Ops:
  0.6 127.8 %shard_map.153 = (f32[1,256,512]{2,1,0:T(8,128)S(1)}, f32[1,256,512]{2,1,0:T(8,128)S(1)}, f32[1,64,2048]{2,1,0:T(8,128)S(1)}, f32[1,256,512]{2,1,0:T(8,128)S(1)}...) custom-call(s32[1,512]{1,0:T(1,128)} %ids.1, f32[1,512]{1,0:T(1,128)} %route.1, ...), custom_call_target="tpu_custom_call" | custom-call | tf_op jit(solution)/shard_map/pallas_call | solution.py:717
  128.4 3.1 %shard_map.154 = (f32[1,256,512]{2,1,0:T(8,128)}, f32[1,256,512]{2,1,0:T(8,128)}, f32[1,64,2048]{2,1,0:T(8,128)}, f32[1,256,512]{2,1,0:T(8,128)}, f32[1,256,512]...) custom-call(f32[1,256,512]{2,1,0:T(8,128)S(1)} %get-tuple-element.14.refs_0_, ...), custom_call_target="tpu_custom_call" | custom-call | tf_op jit(solution)/shard_map/pallas_call | solution.py:763

commit v4 on v3

--- a/solution.py
+++ b/solution.py
@@ -182,22 +182,39 @@
 
     lane = lax.broadcasted_iota(jnp.int32, (slots, 128), 1)
 
-    def chosen(d):
-        column = jnp.transpose(jnp.broadcast_to(all_ids[d], (128, slots)))
+    def chosen(d, first=0, count=slots):
+        column = jnp.transpose(jnp.broadcast_to(all_ids[d][:, first : first + count], (128, count)))
         return jnp.concatenate(
-            [jnp.where(column == lane + c * 128, 1.0, 0.0).astype(bf16) for c in range(pool_rows // 128)], axis=1
+            [jnp.where(column == lane[:count] + c * 128, 1.0, 0.0).astype(bf16) for c in range(pool_rows // 128)],
+            axis=1,
         )
 
     own_cols = block(me_e, width)
+    pieces = ((0, slots // 4), (slots // 4, slots - slots // 4))
+
+    def tokens_out(d, i):
+        at = pl.ds(*pieces[i])
+        stage_x[d - 1, at, :] = dot(chosen(d, *pieces[i]), tokens[...]).astype(bf16)
+        send(
+            stage_x.at[d - 1, at], routed.at[at, own_cols], tok_send.at[d, i], tok_recv.at[d, i], {"expert": me_e ^ d}
+        )
+
     loads[3].wait()
-    for d in peers_e:
-        id_copies[d].wait_recv()
-        stage_x[d - 1] = dot(chosen(d), tokens[...]).astype(bf16)
-        send(stage_x.at[d - 1], routed.at[:, own_cols], tok_send.at[d, 0], tok_recv.at[d, 0], {"expert": me_e ^ d})
+    near = [d for d in range(1, n_e) if d & (d - 1) == 0]
+    for i in (0, 1):
+        for d in near:
+            if i == 0:
+                id_copies[d].wait_recv()
+            tokens_out(d, i)
+    for d in range(1, n_e):
+        if d not in near:
+            id_copies[d].wait_recv()
+            tokens_out(d, 0)
+            tokens_out(d, 1)
     loads[4].wait()
-    for d in peers_e:
+    for d in range(1, n_e):
         stage_c[d - 1] = dot(chosen(d), cot[...]).astype(bf16)
-        send(stage_c.at[d - 1], cot_rows.at[:, own_cols], tok_send.at[d, 1], tok_recv.at[d, 1], {"expert": me_e ^ d})
+        send(stage_c.at[d - 1], cot_rows.at[:, own_cols], tok_send.at[d, 2], tok_recv.at[d, 2], {"expert": me_e ^ d})
 
     last_hop = chips - 1
     forward(0, 0)
@@ -209,12 +226,17 @@
     route_column = jnp.transpose(jnp.broadcast_to(route[...], (128, slots)))
 
     def tokens_in(d, part):
-        land = (routed, cot_rows)[part]
-        theirs = block(me_e ^ d, width)
-        stage = (stage_x, stage_c)[part]
-        remote(
-            stage.at[d - 1], land.at[:, theirs], tok_send.at[d, part], tok_recv.at[d, part], {"expert": me_e ^ d}
-        ).wait_recv()
+        theirs, peer = block(me_e ^ d, width), {"expert": me_e ^ d}
+        if part:
+            remote(
+                stage_c.at[d - 1], cot_rows.at[:, theirs], tok_send.at[d, 2], tok_recv.at[d, 2], peer
+            ).wait_recv()
+            return
+        for i in (0, 1):
+            at = pl.ds(*pieces[i])
+            remote(
+                stage_x.at[d - 1, at], routed.at[at, theirs], tok_send.at[d, i], tok_recv.at[d, i], peer
+            ).wait_recv()
 
     def turn(d):
         e = me_e ^ d
@@ -249,12 +271,15 @@
 
     turn(0)
     scale(0)
-    for d in peers_e:
+    for d in range(1, n_e):
         tokens_in(d, 0)
         turn(d)
     crossed(0, 0)
     multiply(chip, True)
     for hop in range(1, chips):
+        if hop == last_hop:
+            tokens_in(1, 1)
+            scale(1)
         if hop > 1:
             forward(hop - 1, 0)
         multiply_hop(hop)
@@ -323,12 +348,15 @@
 
     down_copies = {}
 
-    def gradient_down(d):
+    def down_away(d):
         at = block(me_e ^ d, width)
         sent[DOWN][:, at] = (dot(h_t[1], cot_rows[:, at]) * (1.0 / slots)).astype(bf16)
         down_copies[d] = send(
             sent[DOWN].at[:, at], ins[DOWN][0].at[:, at], dn_send.at[d], dn_recv.at[d], {"dp": me ^ 1}
         )
+
+    def down_own(d):
+        at = block(me_e ^ d, width)
         own[DOWN][:, at] = dot(h_t[0], cot_rows[:, at]) * (1.0 / slots)
 
     def low(t):
@@ -364,7 +392,7 @@
             return ab, aa, bb
 
         if m == DOWN and t == 0:
-            for d in (0, *peers_e):
+            for d in range(n_e):
                 down_copies[d].wait_recv()
                 first = (me_e ^ d) * width
                 places = [pl.ds(pl.multiple_of(first + c, lump), lump) for c in range(0, width, lump)]
@@ -421,7 +449,7 @@
         n = count * steps
         lax.fori_loop(0, n, body, 0, unroll=2 if n % 2 == 0 else 1)
 
-    def merge(m, t):
+    def merge(m, t, then=None):
         c_m, c_o = settle(m, t)
         up = bit_of(t + 1)
         count = blocks_at(t + 1)
@@ -433,6 +461,8 @@
             own[m][at, to] = value
 
         combine(m, t, c_m, c_o, count, lambda j: 2 * j + 1 - up, store_away)
+        if then is not None:
+            then()
         combine(m, t, c_m, c_o, count, lambda j: 2 * j + up, store_own)
 
     new, following = (new_gate, new_up, new_down), (next_gate, next_up, next_down)
@@ -460,7 +490,7 @@
 
     def scatter(m):
         c_m, c_o = settle(m, 0)
-        for r in (3, 2, 1):
+        for r in (2, 3, 1):
             def store_far(i, at, to, value, r=r):
                 far_out[pl.ds(pl.multiple_of((r - 1) * rows[m] + i * step, step), step), to] = value.astype(bf16)
 
@@ -469,9 +499,8 @@
             far[r] = remote(far_out.at[at], far_in.at[at], far_send.at[r - 1], far_recv.at[r - 1], {"dp": me ^ (2 * r)})
             pending.append(far[r])
             if r == 3:
-                far[r].start()
-            elif r == 2:
-                pl.when(other_way)(far[r].start)
+                pl.when(other_way)(far[2].start)
+                far[3].start()
 
         def store_own(i, at, to, value):
             own[m][at, to] = value
@@ -549,31 +578,30 @@
 
         lax.fori_loop(0, rows[m] // step, body, 0, unroll=2)
 
-    gradient_down(0)
-    for d in peers_e:
-        tokens_in(d, 1)
-        scale(d)
-        gradient_down(d)
+    down_away(0)
+    for d in range(1, n_e):
+        if d > 1:
+            tokens_in(d, 1)
+            scale(d)
+        down_away(d)
+    for d in range(n_e):
+        down_own(d)
     forward(last_hop - 1, 1)
     measure(DOWN, 0)
-    for hop in range(chips):
-        crossed(hop, 1)
-
-    def backward(m):
-        at = slice(m * tall, (m + 1) * tall)
-        back = dot_t(cot_rows[at, :], dn_full[...])
-        both[at, :hid] = (back * pre[at, :hid]).astype(bf16)
-        both[at, hid:] = (back * pre[at, hid:]).astype(bf16)
-
-    backward(0)
     straight = chips == 4
     if straight:
         scatter(DOWN)
     else:
         merge(DOWN, 0)
         launch_all(DOWN, 1)
-    for m in range(1, slots // tall):
-        backward(m)
+
+    for hop in range(chips):
+        crossed(hop, 1)
+    for m in range(slots // tall):
+        at = slice(m * tall, (m + 1) * tall)
+        back = dot_t(cot_rows[at, :], dn_full[...])
+        both[at, :hid] = (back * pre[at, :hid]).astype(bf16)
+        both[at, hid:] = (back * pre[at, hid:]).astype(bf16)
 
     def slot_back(d):
         weight = gu_full[block(me_e ^ d, width), :]
@@ -602,14 +630,17 @@
             pool[pl.ds(at, tile), :] = dot(pick, returned[...])
 
     gradient(GATE, True)
+    gradient(GATE, False)
     gradient(UP, True)
-    gradient(GATE, False)
+    gradient(UP, False)
     measure(GATE, 0)
-    gradient(UP, False)
-    merge(GATE, 0)
-    if straight:
-        launch_all(GATE, 1)
-        pl.when(same_way)(far[2].start)
+
+    def first_gate():
+        if straight:
+            launch_all(GATE, 1)
+            pl.when(same_way)(far[2].start)
+
+    merge(GATE, 0, first_gate)
     measure(UP, 0)
     back_copies = [slot_back(d) for d in peers_e]
     merge(UP, 0)
@@ -617,18 +648,16 @@
     if straight:
         measure(GATE, 1)
         launch_all(UP, 1)
-        merge(GATE, 1)
-        launch_all(GATE, 2)
+        merge(GATE, 1, lambda: launch_all(GATE, 2))
         measure(UP, 1)
         pl.when(other_way)(far[1].start)
-        measure(GATE, 2)
-        merge(UP, 1)
-        launch_all(UP, 2)
+        merge(UP, 1, lambda: launch_all(UP, 2))
         pl.when(same_way)(far[1].start)
         pool_sum()
-        finish(GATE)
+        measure(GATE, 2)
         gram(DOWN)
         measure(UP, 2)
+        finish(GATE)
         finish_far(DOWN)
         finish(UP)
     else:
@@ -748,7 +777,7 @@
             buf((3 * rows_dn, full), bf16),
             buf((16, 128), f32),
             buf((7, 16, 128), f32),
-            dma((8,)), dma((n_e,)), dma((n_e,)), dma((n_e, 2)), dma((n_e, 2)),
+            dma((8,)), dma((n_e,)), dma((n_e,)), dma((n_e, 3)), dma((n_e, 3)),
             dma((2, chips, 2)), dma((2, chips, 2)), dma((2, chips, 2)), dma((2, chips, 2)),
             dma((n_e,)), dma((n_e,)), dma((3, tiers, 2)), dma((3, tiers, 2)), dma((3, n_stats)), dma((3, n_stats)), dma((n_e,)), dma((n_e,)),
             dma((3,)), dma((3,)), dma((7,)), dma((7,)),

time: 132 us -> 129 us (0.977)
  Pallas kernels: 131 us -> 128 us
    pallas_call x1, Pallas kernels: 128 us -> 124 us  [local(): pl.pallas_call(functools.partial(step_kernel, n_e, n_dp), out_shape=[buf(...]
where the time goes in v4:
time: 129 us; the launch traced here: 128 us
  Pallas kernels  128 us (99%)
    pallas_call x1, Pallas kernels, local(): pl.pallas_call(functools.partial(step_kernel, n_e, n_dp), out_shape=[buf(...  124 us
    pallas_call x1, Pallas kernels, local(): pl.pallas_call(store_kernel, out_shape=[jax.ShapeDtypeStruct(*x) for x in...  3.11 us

profile of v4, /device:TPU:0, one launch (start us, length us, event | category | flops | bytes accessed | tf_op | source)
XLA Modules:
  0.0 128.4 jit_solution(11984904294190660567)
XLA Ops:
  0.6 124.5 %shard_map.153 = (f32[1,256,512]{2,1,0:T(8,128)S(1)}, f32[1,256,512]{2,1,0:T(8,128)S(1)}, f32[1,64,2048]{2,1,0:T(8,128)S(1)}, f32[1,256,512]{2,1,0:T(8,128)S(1)}...) custom-call(s32[1,512]{1,0:T(1,128)} %ids.1, f32[1,512]{1,0:T(1,128)} %route.1, ...), custom_call_target="tpu_custom_call" | custom-call | tf_op jit(solution)/shard_map/pallas_call | solution.py:746
  125.1 3.1 %shard_map.154 = (f32[1,256,512]{2,1,0:T(8,128)}, f32[1,256,512]{2,1,0:T(8,128)}, f32[1,64,2048]{2,1,0:T(8,128)}, f32[1,256,512]{2,1,0:T(8,128)}, f32[1,256,512]...) custom-call(f32[1,256,512]{2,1,0:T(8,128)S(1)} %get-tuple-element.14.refs_0_, ...), custom_call_target="tpu_custom_call" | custom-call | tf_op jit(solution)/shard_map/pallas_call | solution.py:792

commit v5 on v4

--- a/solution.py
+++ b/solution.py
@@ -52,8 +52,12 @@
     barrier = pltpu.get_barrier_semaphore()
     for d in range(1, n_e):
         pl.semaphore_signal(barrier, inc=1, device_id={"expert": me_e ^ d}, device_id_type=MESH)
-    for d in range(1, n_dp):
-        pl.semaphore_signal(barrier, inc=1, device_id={"dp": me ^ d}, device_id_type=MESH)
+    pl.semaphore_signal(barrier, inc=1, device_id={"dp": me ^ 1}, device_id_type=MESH)
+    ends = (chip < chips - 1, chip >= 1)
+    for way, there in zip((1, -1), ends):
+        @pl.when(there)
+        def _(way=way):
+            pl.semaphore_signal(barrier, inc=1, device_id={"dp": me + 2 * way}, device_id_type=MESH)
 
     loads = [
         pltpu.make_async_copy(src, dst, in_sem.at[i])
@@ -98,7 +102,7 @@
     loads[2].wait()
     dn_full[mine_dn, :] = weights[DOWN][...].astype(bf16)
 
-    pl.semaphore_wait(barrier, n_e + n_dp - 2)
+    pl.semaphore_wait(barrier, n_e + jnp.where(ends[0], 1, 0) + jnp.where(ends[1], 1, 0))
 
     id_copies = [None] + [
         send(ids, all_ids.at[d], id_send.at[d], id_recv.at[d], {"expert": me_e ^ d}) for d in range(1, n_e)
@@ -417,8 +421,8 @@
                 stats.at[m, t], stats_in.at[m, offset[t] + d - 1],
                 st_send.at[m, offset[t] + d - 1], st_recv.at[m, offset[t] + d - 1], {"dp": me ^ d},
             )
-            for d in range(1, 2 << t)
-        ]
+            for d in range((2 << t) - 1, 0, -1)
+        ][::-1]
 
     def settle(m, t):
         total = totals[m, t]
@@ -543,8 +547,8 @@
         totals[m, 1] = local
         news[m, 1] = [
             send(far_stats, far_stats_in.at[d - 1], table_send.at[d - 1], table_recv.at[d - 1], {"dp": me ^ d})
-            for d in range(1, n_dp)
-        ]
+            for d in range(n_dp - 1, 0, -1)
+        ][::-1]
 
     def finish_far(m):
         total = totals[m, 1]

time: 129 us -> 128 us (level)
  no operation moved by 1% of the time
where the time goes in v5:
time: 128 us
  Pallas kernels  127 us (99%)
    pallas_call x1, Pallas kernels, local(): pl.pallas_call(functools.partial(step_kernel, n_e, n_dp), out_shape=[buf(...  124 us
    pallas_call x1, Pallas kernels, local(): pl.pallas_call(store_kernel, out_shape=[jax.ShapeDtypeStruct(*x) for x in...  3.11 us

profile of v5, /device:TPU:0, one launch (start us, length us, event | category | flops | bytes accessed | tf_op | source)
XLA Modules:
  0.0 128.3 jit_solution(17219444236337562123)
XLA Ops:
  0.6 124.4 %shard_map.153 = (f32[1,256,512]{2,1,0:T(8,128)S(1)}, f32[1,256,512]{2,1,0:T(8,128)S(1)}, f32[1,64,2048]{2,1,0:T(8,128)S(1)}, f32[1,256,512]{2,1,0:T(8,128)S(1)}...) custom-call(s32[1,512]{1,0:T(1,128)} %ids.1, f32[1,512]{1,0:T(1,128)} %route.1, ...), custom_call_target="tpu_custom_call" | custom-call | tf_op jit(solution)/shard_map/pallas_call | solution.py:750
  125.0 3.1 %shard_map.154 = (f32[1,256,512]{2,1,0:T(8,128)}, f32[1,256,512]{2,1,0:T(8,128)}, f32[1,64,2048]{2,1,0:T(8,128)}, f32[1,256,512]{2,1,0:T(8,128)}, f32[1,256,512]...) custom-call(f32[1,256,512]{2,1,0:T(8,128)S(1)} %get-tuple-element.14.refs_0_, ...), custom_call_target="tpu_custom_call" | custom-call | tf_op jit(solution)/shard_map/pallas_call | solution.py:796
